TPU v7x, 128 devices: a whole 4x4x4 slice. The times are simulated.
128 devices in a mesh: prow: 8 (over y, core), pcol: 16 (over z, x).
Axes of the slice: x: 4, y: 4, z: 4, core: 2. Of those that a mesh axis runs over, the one named last changes fastest.
Arguments:
- inverse_cov: bfloat16 [8192, 8192], P('prow', 'pcol'), may hold values from -0.5 to 4.5, as said below
- cosines: float32 [8192, 8192], P('prow', 'pcol'), may hold values from -1 to 1, as said below
- sky_maps: bfloat16 [8192, 192], P('pcol'), may hold values from -6 to 6
Outputs:
- filtered: bfloat16 [8192, 192], P('prow')
- spectra: float32 [64, 192], replicated
Inputs may be any that keep to these rules, and one draw needn't show every extreme that they name: `inverse_cov`: symmetric, with a dominant diagonal. `cosines`: symmetric.
All inputs are finite; a program needn't handle non-finite values.
Results may differ from a plain program's by a relative error of at most 0.0033.
Values may be sent and summed in bfloat16 or wider, within the bound.
No kernel may reach another device: no remote copies, remote signals or barrier semaphores. Data moves between devices by JAX's collectives and lax.ppermute only.
A program may use at most 64 MiB of HBM per device.

v0:
```python
import jax
import jax.numpy as jnp
from jax import lax
from jax.sharding import Mesh
from jax.sharding import PartitionSpec as P

NPIX = 8192
L = 64
LMIN = 2
GROUP = 4
PCOL = ("pcol_0", "pcol_1")
PROW = ("prow_0", "prow_1")
PROW_PCOL = ("prow_0", "prow_1", "pcol_0", "pcol_1")


def split_up(value, dim, length):
    dims = value.shape
    parts = value.reshape(*dims[:dim], length, dims[dim] // length, *dims[dim + 1 :])
    return jnp.moveaxis(parts, dim, 0)


def summed_on_arrival(value, axis, dim):
    length = lax.axis_size(axis)
    parts = lax.all_to_all(split_up(value, dim, length), axis, 0, 0, tiled=True)
    return jnp.sum(parts, axis=0)


def from_everyone(value, axis):
    length = lax.axis_size(axis)
    return lax.all_to_all(
        jnp.broadcast_to(value[None], (length, *value.shape)), axis, 0, 0, tiled=True
    )


def joined_along(parts, dim):
    parts = jnp.moveaxis(parts, 0, dim)
    dims = parts.shape
    return parts.reshape(*dims[:dim], dims[dim] * dims[dim + 1], *dims[dim + 2 :])


def collect(value, axis, dim):
    parts = from_everyone(value, axis)
    return joined_along(parts, dim)


def broadcast(value, axis, root):
    return lax.dynamic_index_in_dim(lax.all_gather(value, axis), root, 0, keepdims=False)


def by_axis(value, axes):
    for axis in axes:
        value = lax.psum(value, axis)
    return value


def next_legendre(previous, current, cosine, degree):
    return ((2.0 * degree - 1.0) * cosine * current - (degree - 1.0) * previous) / degree


def per_device(inverse_cov, cosines, sky_maps):
    cols_here = inverse_cov.shape[1]
    own_rows = summed_on_arrival(
        jnp.dot(inverse_cov, sky_maps, preferred_element_type=jnp.float32), PCOL, 0
    ).astype(jnp.bfloat16)
    filtered = collect(own_rows, PCOL, 0)
    column_index = lax.axis_index(PCOL)
    col_ratio = lax.axis_size(PCOL) // lax.axis_size(PROW)
    owner_row = column_index // col_ratio
    source = broadcast(filtered, PROW, owner_row)
    filtered_cols = lax.dynamic_slice_in_dim(
        source, column_index % col_ratio * cols_here, cols_here, 0
    )
    rows_f32 = filtered.astype(jnp.float32)
    previous = jnp.ones_like(cosines)
    current = cosines

    def advance(carried, turn_index):
        previous, current = carried
        term_list = []
        weights = []
        for offset in range(GROUP):
            degree = (LMIN + turn_index * GROUP + offset).astype(jnp.float32)
            next_term = next_legendre(previous, current, cosines, degree)
            term_list.append(next_term.astype(jnp.bfloat16))
            weights.append((2.0 * degree + 1.0) / NPIX)
            previous, current = (current, next_term)
        stacked = jnp.stack(term_list)
        product = jnp.einsum(
            "grc,cm->grm", stacked, filtered_cols, preferred_element_type=jnp.float32
        )
        quadratic = jnp.sum(product * rows_f32[None], axis=1)
        return ((previous, current), quadratic * jnp.stack(weights)[:, None])

    carried, partial_spectra = lax.scan(
        advance, (previous, current), jnp.arange(L // GROUP, dtype=jnp.int32)
    )
    spectra = by_axis(partial_spectra.reshape(L, -1), PROW_PCOL)
    return (filtered, spectra)


def solution(mesh):
    split = Mesh(mesh.devices.reshape(4, 2, 4, 4), ("prow_0", "prow_1", "pcol_0", "pcol_1"))
    placed = (P(PROW, PCOL), P(PROW, PCOL), P(PCOL, None))
    return jax.shard_map(
        per_device, mesh=split, in_specs=placed, out_specs=(P(PROW, None), P()), check_vma=False
    )
```

profile of v0, /device:TPU:0, one launch (start us, length us, event | category | flops | bytes accessed | tf_op | source)
XLA Modules:
  0.0 353.4 jit_solution(7335706579062819510)
XLA Ops:
  9.8 24.9 %all_to_all.10 = f32[16,64,192]{2,1,0:T(8,128)S(1)} all-to-all(f32[16,64,192]{2,1,0:T(8,128)S(1)} %bitcast.57), channel_id=1, replica_groups=mesh['prow_0'=4,'prow_1'=2,'pcol_0'=4,'pcol_1'=4] {'pcol_0','pcol_1'}, dimensions={0} | all-to-all | bytes 1572864 | tf_op jit(solution)/shard_map/all_to_all | solution.py:24
  34.8 13.7 %all_to_all.11 = bf16[16,64,192]{2,1,0:T(8,128)(2,1)S(1)} all-to-all(bf16[16,64,192]{2,1,0:T(8,128)(2,1)S(1)} %broadcast_in_dim.7), channel_id=1, replica_groups=mesh['prow_0'=4,'prow_1'=2,'pcol_0'=4,'pcol_1'=4] {'pcol_0','pcol_1'}, dimensions={0} | all-to-all | bytes 786432 | tf_op jit(solution)/shard_map/all_to_all | solution.py:30
  50.6 2.3 bitcast_convert_fusion
  52.8 2.5 copy.14
  55.3 19.7 %all-gather.2.cloned.1.call-done = bf16[8,1024,192]{1,2,0:T(8,128)(2,1)} async-done(((bf16[1,1024,192]{1,2,0:T(8,128)(2,1)}), bf16[8,1024,192]{1,2,0:T(8,128)(2,1)}) %all-gather.2.cloned.1.call-update) | async-done | bytes 3145744 | tf_op jit(solution)/shard_map/all_gather | solution.py:47
  76.1 214.6 %while.18 = (s32[]{:T(128)}, f32[1024,512]{1,0:T(8,128)}, f32[1024,512]{1,0:T(8,128)S(1)}, f32[16,4,192]{2,1,0:T(4,128)S(1)}, s32[16]{0:T(128)S(1)}, /*index=5*/...) while((s32[]{:T(128)}, f32[1024,512]{1,0:T(8,128)}, ...), condition=%wide.region_3.4_spmd.clone, body=%wide.region_1.3_spmd.clone.sunk | while | flops 832045056 | bytes 69153048 | solution.py:94
  77.6 3.5 %convert_bitcast_fusion.6 = (bf16[1,1024,512]{2,1,0:T(8,128)(2,1)S(1)}, f32[1024,512]{1,0:T(8,128)S(1)}, bf16[1,1024,512]{2,1,0:T(8,128)(2,1)S(1)}) fusion(f32[]{:T(128)} %bitcast.47, f32[]{:T(128)S(6)} %sub.103, f32[]{:T(128)} %bitcast.48, f32[1024,512]{1,0:T(8,128)} %copy-done.2, f32[]{:T(128)S(6)} %sub.104, f32[]{:T(128)} %bitcast.49, ...), kind=kLoop, calls=%fused_computation.16.clone.1 | loop fusion | flops 9437184 | bytes 10485797 | tf_op jit(solution)/shard_map/while/body/eval_jaxpr/stack | solution.py:87
  81.1 4.1 %convert_bitcast_fusion.7 = (bf16[1,1024,512]{2,1,0:T(8,128)(2,1)S(1)}, f32[1024,512]{1,0:T(8,128)}, bf16[1,1024,512]{2,1,0:T(8,128)(2,1)S(1)}) fusion(f32[]{:T(128)} %bitcast.50, f32[]{:T(128)} %bitcast.48, f32[1024,512]{1,0:T(8,128)} %copy-done.2, f32[]{:T(128)S(6)} %sub.104, f32[]{:T(128)} %bitcast.49, f32[1024,512]{1,0:T(8,128)S(1)} %copy-done.5, ...), kind=kLoop, calls=%fused_computation.15.clone.1 | loop fusion | flops 9437184 | bytes 12582949 | tf_op jit(solution)/shard_map/while/body/eval_jaxpr/stack | solution.py:87
  90.4 4.2 %convert_bitcast_fusion.6 = (bf16[1,1024,512]{2,1,0:T(8,128)(2,1)S(1)}, f32[1024,512]{1,0:T(8,128)S(1)}, bf16[1,1024,512]{2,1,0:T(8,128)(2,1)S(1)}) fusion(f32[]{:T(128)} %bitcast.47, f32[]{:T(128)S(6)} %sub.103, f32[]{:T(128)} %bitcast.48, f32[1024,512]{1,0:T(8,128)} %copy-done.2, f32[]{:T(128)S(6)} %sub.104, f32[]{:T(128)} %bitcast.49, ...), kind=kLoop, calls=%fused_computation.16.clone.1 | loop fusion | flops 9437184 | bytes 10485797 | tf_op jit(solution)/shard_map/while/body/eval_jaxpr/stack | solution.py:87
  94.6 4.1 %convert_bitcast_fusion.7 = (bf16[1,1024,512]{2,1,0:T(8,128)(2,1)S(1)}, f32[1024,512]{1,0:T(8,128)}, bf16[1,1024,512]{2,1,0:T(8,128)(2,1)S(1)}) fusion(f32[]{:T(128)} %bitcast.50, f32[]{:T(128)} %bitcast.48, f32[1024,512]{1,0:T(8,128)} %copy-done.2, f32[]{:T(128)S(6)} %sub.104, f32[]{:T(128)} %bitcast.49, f32[1024,512]{1,0:T(8,128)S(1)} %copy-done.5, ...), kind=kLoop, calls=%fused_computation.15.clone.1 | loop fusion | flops 9437184 | bytes 12582949 | tf_op jit(solution)/shard_map/while/body/eval_jaxpr/stack | solution.py:87
  103.8 4.2 %convert_bitcast_fusion.6 = (bf16[1,1024,512]{2,1,0:T(8,128)(2,1)S(1)}, f32[1024,512]{1,0:T(8,128)S(1)}, bf16[1,1024,512]{2,1,0:T(8,128)(2,1)S(1)}) fusion(f32[]{:T(128)} %bitcast.47, f32[]{:T(128)S(6)} %sub.103, f32[]{:T(128)} %bitcast.48, f32[1024,512]{1,0:T(8,128)} %copy-done.2, f32[]{:T(128)S(6)} %sub.104, f32[]{:T(128)} %bitcast.49, ...), kind=kLoop, calls=%fused_computation.16.clone.1 | loop fusion | flops 9437184 | bytes 10485797 | tf_op jit(solution)/shard_map/while/body/eval_jaxpr/stack | solution.py:87
  108.0 4.1 %convert_bitcast_fusion.7 = (bf16[1,1024,512]{2,1,0:T(8,128)(2,1)S(1)}, f32[1024,512]{1,0:T(8,128)}, bf16[1,1024,512]{2,1,0:T(8,128)(2,1)S(1)}) fusion(f32[]{:T(128)} %bitcast.50, f32[]{:T(128)} %bitcast.48, f32[1024,512]{1,0:T(8,128)} %copy-done.2, f32[]{:T(128)S(6)} %sub.104, f32[]{:T(128)} %bitcast.49, f32[1024,512]{1,0:T(8,128)S(1)} %copy-done.5, ...), kind=kLoop, calls=%fused_computation.15.clone.1 | loop fusion | flops 9437184 | bytes 12582949 | tf_op jit(solution)/shard_map/while/body/eval_jaxpr/stack | solution.py:87
  113.8 1.9 multiply_reduce_fusion.2
  117.3 4.2 %convert_bitcast_fusion.6 = (bf16[1,1024,512]{2,1,0:T(8,128)(2,1)S(1)}, f32[1024,512]{1,0:T(8,128)S(1)}, bf16[1,1024,512]{2,1,0:T(8,128)(2,1)S(1)}) fusion(f32[]{:T(128)} %bitcast.47, f32[]{:T(128)S(6)} %sub.103, f32[]{:T(128)} %bitcast.48, f32[1024,512]{1,0:T(8,128)} %copy-done.2, f32[]{:T(128)S(6)} %sub.104, f32[]{:T(128)} %bitcast.49, ...), kind=kLoop, calls=%fused_computation.16.clone.1 | loop fusion | flops 9437184 | bytes 10485797 | tf_op jit(solution)/shard_map/while/body/eval_jaxpr/stack | solution.py:87
  121.5 4.1 %convert_bitcast_fusion.7 = (bf16[1,1024,512]{2,1,0:T(8,128)(2,1)S(1)}, f32[1024,512]{1,0:T(8,128)}, bf16[1,1024,512]{2,1,0:T(8,128)(2,1)S(1)}) fusion(f32[]{:T(128)} %bitcast.50, f32[]{:T(128)} %bitcast.48, f32[1024,512]{1,0:T(8,128)} %copy-done.2, f32[]{:T(128)S(6)} %sub.104, f32[]{:T(128)} %bitcast.49, f32[1024,512]{1,0:T(8,128)S(1)} %copy-done.5, ...), kind=kLoop, calls=%fused_computation.15.clone.1 | loop fusion | flops 9437184 | bytes 12582949 | tf_op jit(solution)/shard_map/while/body/eval_jaxpr/stack | solution.py:87
  127.3 1.9 multiply_reduce_fusion.2
  130.7 4.2 %convert_bitcast_fusion.6 = (bf16[1,1024,512]{2,1,0:T(8,128)(2,1)S(1)}, f32[1024,512]{1,0:T(8,128)S(1)}, bf16[1,1024,512]{2,1,0:T(8,128)(2,1)S(1)}) fusion(f32[]{:T(128)} %bitcast.47, f32[]{:T(128)S(6)} %sub.103, f32[]{:T(128)} %bitcast.48, f32[1024,512]{1,0:T(8,128)} %copy-done.2, f32[]{:T(128)S(6)} %sub.104, f32[]{:T(128)} %bitcast.49, ...), kind=kLoop, calls=%fused_computation.16.clone.1 | loop fusion | flops 9437184 | bytes 10485797 | tf_op jit(solution)/shard_map/while/body/eval_jaxpr/stack | solution.py:87
  134.9 4.1 %convert_bitcast_fusion.7 = (bf16[1,1024,512]{2,1,0:T(8,128)(2,1)S(1)}, f32[1024,512]{1,0:T(8,128)}, bf16[1,1024,512]{2,1,0:T(8,128)(2,1)S(1)}) fusion(f32[]{:T(128)} %bitcast.50, f32[]{:T(128)} %bitcast.48, f32[1024,512]{1,0:T(8,128)} %copy-done.2, f32[]{:T(128)S(6)} %sub.104, f32[]{:T(128)} %bitcast.49, f32[1024,512]{1,0:T(8,128)S(1)} %copy-done.5, ...), kind=kLoop, calls=%fused_computation.15.clone.1 | loop fusion | flops 9437184 | bytes 12582949 | tf_op jit(solution)/shard_map/while/body/eval_jaxpr/stack | solution.py:87
  140.7 1.9 multiply_reduce_fusion.2
  144.2 4.2 %convert_bitcast_fusion.6 = (bf16[1,1024,512]{2,1,0:T(8,128)(2,1)S(1)}, f32[1024,512]{1,0:T(8,128)S(1)}, bf16[1,1024,512]{2,1,0:T(8,128)(2,1)S(1)}) fusion(f32[]{:T(128)} %bitcast.47, f32[]{:T(128)S(6)} %sub.103, f32[]{:T(128)} %bitcast.48, f32[1024,512]{1,0:T(8,128)} %copy-done.2, f32[]{:T(128)S(6)} %sub.104, f32[]{:T(128)} %bitcast.49, ...), kind=kLoop, calls=%fused_computation.16.clone.1 | loop fusion | flops 9437184 | bytes 10485797 | tf_op jit(solution)/shard_map/while/body/eval_jaxpr/stack | solution.py:87
  148.4 4.1 %convert_bitcast_fusion.7 = (bf16[1,1024,512]{2,1,0:T(8,128)(2,1)S(1)}, f32[1024,512]{1,0:T(8,128)}, bf16[1,1024,512]{2,1,0:T(8,128)(2,1)S(1)}) fusion(f32[]{:T(128)} %bitcast.50, f32[]{:T(128)} %bitcast.48, f32[1024,512]{1,0:T(8,128)} %copy-done.2, f32[]{:T(128)S(6)} %sub.104, f32[]{:T(128)} %bitcast.49, f32[1024,512]{1,0:T(8,128)S(1)} %copy-done.5, ...), kind=kLoop, calls=%fused_computation.15.clone.1 | loop fusion | flops 9437184 | bytes 12582949 | tf_op jit(solution)/shard_map/while/body/eval_jaxpr/stack | solution.py:87
  154.2 1.9 multiply_reduce_fusion.2
  157.6 4.2 %convert_bitcast_fusion.6 = (bf16[1,1024,512]{2,1,0:T(8,128)(2,1)S(1)}, f32[1024,512]{1,0:T(8,128)S(1)}, bf16[1,1024,512]{2,1,0:T(8,128)(2,1)S(1)}) fusion(f32[]{:T(128)} %bitcast.47, f32[]{:T(128)S(6)} %sub.103, f32[]{:T(128)} %bitcast.48, f32[1024,512]{1,0:T(8,128)} %copy-done.2, f32[]{:T(128)S(6)} %sub.104, f32[]{:T(128)} %bitcast.49, ...), kind=kLoop, calls=%fused_computation.16.clone.1 | loop fusion | flops 9437184 | bytes 10485797 | tf_op jit(solution)/shard_map/while/body/eval_jaxpr/stack | solution.py:87
  161.8 4.1 %convert_bitcast_fusion.7 = (bf16[1,1024,512]{2,1,0:T(8,128)(2,1)S(1)}, f32[1024,512]{1,0:T(8,128)}, bf16[1,1024,512]{2,1,0:T(8,128)(2,1)S(1)}) fusion(f32[]{:T(128)} %bitcast.50, f32[]{:T(128)} %bitcast.48, f32[1024,512]{1,0:T(8,128)} %copy-done.2, f32[]{:T(128)S(6)} %sub.104, f32[]{:T(128)} %bitcast.49, f32[1024,512]{1,0:T(8,128)S(1)} %copy-done.5, ...), kind=kLoop, calls=%fused_computation.15.clone.1 | loop fusion | flops 9437184 | bytes 12582949 | tf_op jit(solution)/shard_map/while/body/eval_jaxpr/stack | solution.py:87
  167.6 1.9 multiply_reduce_fusion.2
  171.1 4.2 %convert_bitcast_fusion.6 = (bf16[1,1024,512]{2,1,0:T(8,128)(2,1)S(1)}, f32[1024,512]{1,0:T(8,128)S(1)}, bf16[1,1024,512]{2,1,0:T(8,128)(2,1)S(1)}) fusion(f32[]{:T(128)} %bitcast.47, f32[]{:T(128)S(6)} %sub.103, f32[]{:T(128)} %bitcast.48, f32[1024,512]{1,0:T(8,128)} %copy-done.2, f32[]{:T(128)S(6)} %sub.104, f32[]{:T(128)} %bitcast.49, ...), kind=kLoop, calls=%fused_computation.16.clone.1 | loop fusion | flops 9437184 | bytes 10485797 | tf_op jit(solution)/shard_map/while/body/eval_jaxpr/stack | solution.py:87
  175.3 4.1 %convert_bitcast_fusion.7 = (bf16[1,1024,512]{2,1,0:T(8,128)(2,1)S(1)}, f32[1024,512]{1,0:T(8,128)}, bf16[1,1024,512]{2,1,0:T(8,128)(2,1)S(1)}) fusion(f32[]{:T(128)} %bitcast.50, f32[]{:T(128)} %bitcast.48, f32[1024,512]{1,0:T(8,128)} %copy-done.2, f32[]{:T(128)S(6)} %sub.104, f32[]{:T(128)} %bitcast.49, f32[1024,512]{1,0:T(8,128)S(1)} %copy-done.5, ...), kind=kLoop, calls=%fused_computation.15.clone.1 | loop fusion | flops 9437184 | bytes 12582949 | tf_op jit(solution)/shard_map/while/body/eval_jaxpr/stack | solution.py:87
  181.1 1.9 multiply_reduce_fusion.2
  184.5 4.2 %convert_bitcast_fusion.6 = (bf16[1,1024,512]{2,1,0:T(8,128)(2,1)S(1)}, f32[1024,512]{1,0:T(8,128)S(1)}, bf16[1,1024,512]{2,1,0:T(8,128)(2,1)S(1)}) fusion(f32[]{:T(128)} %bitcast.47, f32[]{:T(128)S(6)} %sub.103, f32[]{:T(128)} %bitcast.48, f32[1024,512]{1,0:T(8,128)} %copy-done.2, f32[]{:T(128)S(6)} %sub.104, f32[]{:T(128)} %bitcast.49, ...), kind=kLoop, calls=%fused_computation.16.clone.1 | loop fusion | flops 9437184 | bytes 10485797 | tf_op jit(solution)/shard_map/while/body/eval_jaxpr/stack | solution.py:87
  188.7 4.1 %convert_bitcast_fusion.7 = (bf16[1,1024,512]{2,1,0:T(8,128)(2,1)S(1)}, f32[1024,512]{1,0:T(8,128)}, bf16[1,1024,512]{2,1,0:T(8,128)(2,1)S(1)}) fusion(f32[]{:T(128)} %bitcast.50, f32[]{:T(128)} %bitcast.48, f32[1024,512]{1,0:T(8,128)} %copy-done.2, f32[]{:T(128)S(6)} %sub.104, f32[]{:T(128)} %bitcast.49, f32[1024,512]{1,0:T(8,128)S(1)} %copy-done.5, ...), kind=kLoop, calls=%fused_computation.15.clone.1 | loop fusion | flops 9437184 | bytes 12582949 | tf_op jit(solution)/shard_map/while/body/eval_jaxpr/stack | solution.py:87
  198.0 4.2 %convert_bitcast_fusion.6 = (bf16[1,1024,512]{2,1,0:T(8,128)(2,1)S(1)}, f32[1024,512]{1,0:T(8,128)S(1)}, bf16[1,1024,512]{2,1,0:T(8,128)(2,1)S(1)}) fusion(f32[]{:T(128)} %bitcast.47, f32[]{:T(128)S(6)} %sub.103, f32[]{:T(128)} %bitcast.48, f32[1024,512]{1,0:T(8,128)} %copy-done.2, f32[]{:T(128)S(6)} %sub.104, f32[]{:T(128)} %bitcast.49, ...), kind=kLoop, calls=%fused_computation.16.clone.1 | loop fusion | flops 9437184 | bytes 10485797 | tf_op jit(solution)/shard_map/while/body/eval_jaxpr/stack | solution.py:87
  202.2 4.1 %convert_bitcast_fusion.7 = (bf16[1,1024,512]{2,1,0:T(8,128)(2,1)S(1)}, f32[1024,512]{1,0:T(8,128)}, bf16[1,1024,512]{2,1,0:T(8,128)(2,1)S(1)}) fusion(f32[]{:T(128)} %bitcast.50, f32[]{:T(128)} %bitcast.48, f32[1024,512]{1,0:T(8,128)} %copy-done.2, f32[]{:T(128)S(6)} %sub.104, f32[]{:T(128)} %bitcast.49, f32[1024,512]{1,0:T(8,128)S(1)} %copy-done.5, ...), kind=kLoop, calls=%fused_computation.15.clone.1 | loop fusion | flops 9437184 | bytes 12582949 | tf_op jit(solution)/shard_map/while/body/eval_jaxpr/stack | solution.py:87
  211.4 4.2 %convert_bitcast_fusion.6 = (bf16[1,1024,512]{2,1,0:T(8,128)(2,1)S(1)}, f32[1024,512]{1,0:T(8,128)S(1)}, bf16[1,1024,512]{2,1,0:T(8,128)(2,1)S(1)}) fusion(f32[]{:T(128)} %bitcast.47, f32[]{:T(128)S(6)} %sub.103, f32[]{:T(128)} %bitcast.48, f32[1024,512]{1,0:T(8,128)} %copy-done.2, f32[]{:T(128)S(6)} %sub.104, f32[]{:T(128)} %bitcast.49, ...), kind=kLoop, calls=%fused_computation.16.clone.1 | loop fusion | flops 9437184 | bytes 10485797 | tf_op jit(solution)/shard_map/while/body/eval_jaxpr/stack | solution.py:87
  215.6 4.1 %convert_bitcast_fusion.7 = (bf16[1,1024,512]{2,1,0:T(8,128)(2,1)S(1)}, f32[1024,512]{1,0:T(8,128)}, bf16[1,1024,512]{2,1,0:T(8,128)(2,1)S(1)}) fusion(f32[]{:T(128)} %bitcast.50, f32[]{:T(128)} %bitcast.48, f32[1024,512]{1,0:T(8,128)} %copy-done.2, f32[]{:T(128)S(6)} %sub.104, f32[]{:T(128)} %bitcast.49, f32[1024,512]{1,0:T(8,128)S(1)} %copy-done.5, ...), kind=kLoop, calls=%fused_computation.15.clone.1 | loop fusion | flops 9437184 | bytes 12582949 | tf_op jit(solution)/shard_map/while/body/eval_jaxpr/stack | solution.py:87
  224.9 4.2 %convert_bitcast_fusion.6 = (bf16[1,1024,512]{2,1,0:T(8,128)(2,1)S(1)}, f32[1024,512]{1,0:T(8,128)S(1)}, bf16[1,1024,512]{2,1,0:T(8,128)(2,1)S(1)}) fusion(f32[]{:T(128)} %bitcast.47, f32[]{:T(128)S(6)} %sub.103, f32[]{:T(128)} %bitcast.48, f32[1024,512]{1,0:T(8,128)} %copy-done.2, f32[]{:T(128)S(6)} %sub.104, f32[]{:T(128)} %bitcast.49, ...), kind=kLoop, calls=%fused_computation.16.clone.1 | loop fusion | flops 9437184 | bytes 10485797 | tf_op jit(solution)/shard_map/while/body/eval_jaxpr/stack | solution.py:87
  229.1 4.1 %convert_bitcast_fusion.7 = (bf16[1,1024,512]{2,1,0:T(8,128)(2,1)S(1)}, f32[1024,512]{1,0:T(8,128)}, bf16[1,1024,512]{2,1,0:T(8,128)(2,1)S(1)}) fusion(f32[]{:T(128)} %bitcast.50, f32[]{:T(128)} %bitcast.48, f32[1024,512]{1,0:T(8,128)} %copy-done.2, f32[]{:T(128)S(6)} %sub.104, f32[]{:T(128)} %bitcast.49, f32[1024,512]{1,0:T(8,128)S(1)} %copy-done.5, ...), kind=kLoop, calls=%fused_computation.15.clone.1 | loop fusion | flops 9437184 | bytes 12582949 | tf_op jit(solution)/shard_map/while/body/eval_jaxpr/stack | solution.py:87
  238.3 4.2 %convert_bitcast_fusion.6 = (bf16[1,1024,512]{2,1,0:T(8,128)(2,1)S(1)}, f32[1024,512]{1,0:T(8,128)S(1)}, bf16[1,1024,512]{2,1,0:T(8,128)(2,1)S(1)}) fusion(f32[]{:T(128)} %bitcast.47, f32[]{:T(128)S(6)} %sub.103, f32[]{:T(128)} %bitcast.48, f32[1024,512]{1,0:T(8,128)} %copy-done.2, f32[]{:T(128)S(6)} %sub.104, f32[]{:T(128)} %bitcast.49, ...), kind=kLoop, calls=%fused_computation.16.clone.1 | loop fusion | flops 9437184 | bytes 10485797 | tf_op jit(solution)/shard_map/while/body/eval_jaxpr/stack | solution.py:87
  242.5 4.1 %convert_bitcast_fusion.7 = (bf16[1,1024,512]{2,1,0:T(8,128)(2,1)S(1)}, f32[1024,512]{1,0:T(8,128)}, bf16[1,1024,512]{2,1,0:T(8,128)(2,1)S(1)}) fusion(f32[]{:T(128)} %bitcast.50, f32[]{:T(128)} %bitcast.48, f32[1024,512]{1,0:T(8,128)} %copy-done.2, f32[]{:T(128)S(6)} %sub.104, f32[]{:T(128)} %bitcast.49, f32[1024,512]{1,0:T(8,128)S(1)} %copy-done.5, ...), kind=kLoop, calls=%fused_computation.15.clone.1 | loop fusion | flops 9437184 | bytes 12582949 | tf_op jit(solution)/shard_map/while/body/eval_jaxpr/stack | solution.py:87
  251.8 4.2 %convert_bitcast_fusion.6 = (bf16[1,1024,512]{2,1,0:T(8,128)(2,1)S(1)}, f32[1024,512]{1,0:T(8,128)S(1)}, bf16[1,1024,512]{2,1,0:T(8,128)(2,1)S(1)}) fusion(f32[]{:T(128)} %bitcast.47, f32[]{:T(128)S(6)} %sub.103, f32[]{:T(128)} %bitcast.48, f32[1024,512]{1,0:T(8,128)} %copy-done.2, f32[]{:T(128)S(6)} %sub.104, f32[]{:T(128)} %bitcast.49, ...), kind=kLoop, calls=%fused_computation.16.clone.1 | loop fusion | flops 9437184 | bytes 10485797 | tf_op jit(solution)/shard_map/while/body/eval_jaxpr/stack | solution.py:87
  256.0 4.1 %convert_bitcast_fusion.7 = (bf16[1,1024,512]{2,1,0:T(8,128)(2,1)S(1)}, f32[1024,512]{1,0:T(8,128)}, bf16[1,1024,512]{2,1,0:T(8,128)(2,1)S(1)}) fusion(f32[]{:T(128)} %bitcast.50, f32[]{:T(128)} %bitcast.48, f32[1024,512]{1,0:T(8,128)} %copy-done.2, f32[]{:T(128)S(6)} %sub.104, f32[]{:T(128)} %bitcast.49, f32[1024,512]{1,0:T(8,128)S(1)} %copy-done.5, ...), kind=kLoop, calls=%fused_computation.15.clone.1 | loop fusion | flops 9437184 | bytes 12582949 | tf_op jit(solution)/shard_map/while/body/eval_jaxpr/stack | solution.py:87
  265.2 4.2 %convert_bitcast_fusion.6 = (bf16[1,1024,512]{2,1,0:T(8,128)(2,1)S(1)}, f32[1024,512]{1,0:T(8,128)S(1)}, bf16[1,1024,512]{2,1,0:T(8,128)(2,1)S(1)}) fusion(f32[]{:T(128)} %bitcast.47, f32[]{:T(128)S(6)} %sub.103, f32[]{:T(128)} %bitcast.48, f32[1024,512]{1,0:T(8,128)} %copy-done.2, f32[]{:T(128)S(6)} %sub.104, f32[]{:T(128)} %bitcast.49, ...), kind=kLoop, calls=%fused_computation.16.clone.1 | loop fusion | flops 9437184 | bytes 10485797 | tf_op jit(solution)/shard_map/while/body/eval_jaxpr/stack | solution.py:87
  269.4 4.1 %convert_bitcast_fusion.7 = (bf16[1,1024,512]{2,1,0:T(8,128)(2,1)S(1)}, f32[1024,512]{1,0:T(8,128)}, bf16[1,1024,512]{2,1,0:T(8,128)(2,1)S(1)}) fusion(f32[]{:T(128)} %bitcast.50, f32[]{:T(128)} %bitcast.48, f32[1024,512]{1,0:T(8,128)} %copy-done.2, f32[]{:T(128)S(6)} %sub.104, f32[]{:T(128)} %bitcast.49, f32[1024,512]{1,0:T(8,128)S(1)} %copy-done.5, ...), kind=kLoop, calls=%fused_computation.15.clone.1 | loop fusion | flops 9437184 | bytes 12582949 | tf_op jit(solution)/shard_map/while/body/eval_jaxpr/stack | solution.py:87
  278.6 4.2 %convert_bitcast_fusion.6 = (bf16[1,1024,512]{2,1,0:T(8,128)(2,1)S(1)}, f32[1024,512]{1,0:T(8,128)S(1)}, bf16[1,1024,512]{2,1,0:T(8,128)(2,1)S(1)}) fusion(f32[]{:T(128)} %bitcast.47, f32[]{:T(128)S(6)} %sub.103, f32[]{:T(128)} %bitcast.48, f32[1024,512]{1,0:T(8,128)} %copy-done.2, f32[]{:T(128)S(6)} %sub.104, f32[]{:T(128)} %bitcast.49, ...), kind=kLoop, calls=%fused_computation.16.clone.1 | loop fusion | flops 9437184 | bytes 10485797 | tf_op jit(solution)/shard_map/while/body/eval_jaxpr/stack | solution.py:87
  282.8 4.1 %convert_bitcast_fusion.7 = (bf16[1,1024,512]{2,1,0:T(8,128)(2,1)S(1)}, f32[1024,512]{1,0:T(8,128)}, bf16[1,1024,512]{2,1,0:T(8,128)(2,1)S(1)}) fusion(f32[]{:T(128)} %bitcast.50, f32[]{:T(128)} %bitcast.48, f32[1024,512]{1,0:T(8,128)} %copy-done.2, f32[]{:T(128)S(6)} %sub.104, f32[]{:T(128)} %bitcast.49, f32[1024,512]{1,0:T(8,128)S(1)} %copy-done.5, ...), kind=kLoop, calls=%fused_computation.15.clone.1 | loop fusion | flops 9437184 | bytes 12582949 | tf_op jit(solution)/shard_map/while/body/eval_jaxpr/stack | solution.py:87
  290.7 16.5 %psum.28 = f32[64,192]{1,0:T(8,128)S(1)} all-reduce(f32[64,192]{1,0:T(8,128)S(1)} %reshape.63), channel_id=1, replica_groups=mesh['prow_0'=4,'prow_1'=2,'pcol_0'=4,'pcol_1'=4] {'prow_0'}, use_global_device_ids=true, to_apply=%region_4.5 | all-reduce | flops 12288 | bytes 98304 | tf_op jit(solution)/shard_map/psum | solution.py:52
  307.2 3.6 %psum.29 = f32[64,192]{1,0:T(8,128)S(1)} all-reduce(f32[64,192]{1,0:T(8,128)S(1)} %psum.28), channel_id=1, replica_groups=mesh['prow_0'=4,'prow_1'=2,'pcol_0'=4,'pcol_1'=4] {'prow_1'}, use_global_device_ids=true, to_apply=%region_5.6 | all-reduce | flops 12288 | bytes 98304 | tf_op jit(solution)/shard_map/psum | solution.py:52
  310.8 17.7 %psum.30 = f32[64,192]{1,0:T(8,128)S(1)} all-reduce(f32[64,192]{1,0:T(8,128)S(1)} %psum.29), channel_id=1, replica_groups=mesh['prow_0'=4,'prow_1'=2,'pcol_0'=4,'pcol_1'=4] {'pcol_0'}, use_global_device_ids=true, to_apply=%region_6.7 | all-reduce | flops 12288 | bytes 98304 | tf_op jit(solution)/shard_map/psum | solution.py:52
  328.5 18.0 %psum.31 = f32[64,192]{1,0:T(8,128)} all-reduce(f32[64,192]{1,0:T(8,128)S(1)} %psum.30), channel_id=1, replica_groups=mesh['prow_0'=4,'prow_1'=2,'pcol_0'=4,'pcol_1'=4] {'pcol_1'}, use_global_device_ids=true, to_apply=%region_7.8 | all-reduce | flops 12288 | bytes 98304 | tf_op jit(solution)/shard_map/psum | solution.py:52
  (252 shorter events, 65.4 us)
Async XLA Ops:
  7.2 67.8 %all-gather.2.cloned.1.call-start = ((), (), s32[]{:S(2)}) async-start(), calls=%async_computation.2 | async-start | bytes 3538944 | tf_op jit(solution)/shard_map/all_gather | solution.py:47
  50.6 25.5 %copy-start.4 = (f32[1024,512]{1,0:T(8,128)S(1)}, f32[1024,512]{1,0:T(8,128)}, u32[]{:S(2)}) copy-start(f32[1024,512]{1,0:T(8,128)} %param.6) | copy-start | bytes 6291460
  77.5 3.6 %copy-start.1 = (f32[1024,512]{1,0:T(8,128)S(1)}, f32[1024,512]{1,0:T(8,128)}, u32[]{:S(2)}) copy-start(f32[1024,512]{1,0:T(8,128)} %get-tuple-element.322) | copy-start | bytes 6291460 | tf_op jit(solution)/shard_map/while
  77.5 3.6 %copy-start.5 = (f32[1024,512]{1,0:T(8,128)S(1)}, f32[1024,512]{1,0:T(8,128)}, u32[]{:S(2)}) copy-start(f32[1024,512]{1,0:T(8,128)} %get-tuple-element.300) | copy-start | bytes 6291460 | tf_op jit(solution)/shard_map/while
  90.4 4.2 %copy-start.1 = (f32[1024,512]{1,0:T(8,128)S(1)}, f32[1024,512]{1,0:T(8,128)}, u32[]{:S(2)}) copy-start(f32[1024,512]{1,0:T(8,128)} %get-tuple-element.322) | copy-start | bytes 6291460 | tf_op jit(solution)/shard_map/while
  90.4 4.2 %copy-start.5 = (f32[1024,512]{1,0:T(8,128)S(1)}, f32[1024,512]{1,0:T(8,128)}, u32[]{:S(2)}) copy-start(f32[1024,512]{1,0:T(8,128)} %get-tuple-element.300) | copy-start | bytes 6291460 | tf_op jit(solution)/shard_map/while
  100.4 2.0 copy-start.3
  103.8 4.2 %copy-start.1 = (f32[1024,512]{1,0:T(8,128)S(1)}, f32[1024,512]{1,0:T(8,128)}, u32[]{:S(2)}) copy-start(f32[1024,512]{1,0:T(8,128)} %get-tuple-element.322) | copy-start | bytes 6291460 | tf_op jit(solution)/shard_map/while
  103.8 4.2 %copy-start.5 = (f32[1024,512]{1,0:T(8,128)S(1)}, f32[1024,512]{1,0:T(8,128)}, u32[]{:S(2)}) copy-start(f32[1024,512]{1,0:T(8,128)} %get-tuple-element.300) | copy-start | bytes 6291460 | tf_op jit(solution)/shard_map/while
  113.8 2.0 copy-start.3
  117.3 4.2 %copy-start.1 = (f32[1024,512]{1,0:T(8,128)S(1)}, f32[1024,512]{1,0:T(8,128)}, u32[]{:S(2)}) copy-start(f32[1024,512]{1,0:T(8,128)} %get-tuple-element.322) | copy-start | bytes 6291460 | tf_op jit(solution)/shard_map/while
  117.3 4.2 %copy-start.5 = (f32[1024,512]{1,0:T(8,128)S(1)}, f32[1024,512]{1,0:T(8,128)}, u32[]{:S(2)}) copy-start(f32[1024,512]{1,0:T(8,128)} %get-tuple-element.300) | copy-start | bytes 6291460 | tf_op jit(solution)/shard_map/while
  127.3 2.0 copy-start.3
  130.7 4.2 %copy-start.1 = (f32[1024,512]{1,0:T(8,128)S(1)}, f32[1024,512]{1,0:T(8,128)}, u32[]{:S(2)}) copy-start(f32[1024,512]{1,0:T(8,128)} %get-tuple-element.322) | copy-start | bytes 6291460 | tf_op jit(solution)/shard_map/while
  130.7 4.2 %copy-start.5 = (f32[1024,512]{1,0:T(8,128)S(1)}, f32[1024,512]{1,0:T(8,128)}, u32[]{:S(2)}) copy-start(f32[1024,512]{1,0:T(8,128)} %get-tuple-element.300) | copy-start | bytes 6291460 | tf_op jit(solution)/shard_map/while
  140.7 2.0 copy-start.3
  144.2 4.2 %copy-start.1 = (f32[1024,512]{1,0:T(8,128)S(1)}, f32[1024,512]{1,0:T(8,128)}, u32[]{:S(2)}) copy-start(f32[1024,512]{1,0:T(8,128)} %get-tuple-element.322) | copy-start | bytes 6291460 | tf_op jit(solution)/shard_map/while
  144.2 4.2 %copy-start.5 = (f32[1024,512]{1,0:T(8,128)S(1)}, f32[1024,512]{1,0:T(8,128)}, u32[]{:S(2)}) copy-start(f32[1024,512]{1,0:T(8,128)} %get-tuple-element.300) | copy-start | bytes 6291460 | tf_op jit(solution)/shard_map/while
  154.2 2.0 copy-start.3
  157.6 4.2 %copy-start.1 = (f32[1024,512]{1,0:T(8,128)S(1)}, f32[1024,512]{1,0:T(8,128)}, u32[]{:S(2)}) copy-start(f32[1024,512]{1,0:T(8,128)} %get-tuple-element.322) | copy-start | bytes 6291460 | tf_op jit(solution)/shard_map/while
  157.6 4.2 %copy-start.5 = (f32[1024,512]{1,0:T(8,128)S(1)}, f32[1024,512]{1,0:T(8,128)}, u32[]{:S(2)}) copy-start(f32[1024,512]{1,0:T(8,128)} %get-tuple-element.300) | copy-start | bytes 6291460 | tf_op jit(solution)/shard_map/while
  167.6 2.0 copy-start.3
  171.1 4.2 %copy-start.1 = (f32[1024,512]{1,0:T(8,128)S(1)}, f32[1024,512]{1,0:T(8,128)}, u32[]{:S(2)}) copy-start(f32[1024,512]{1,0:T(8,128)} %get-tuple-element.322) | copy-start | bytes 6291460 | tf_op jit(solution)/shard_map/while
  171.1 4.2 %copy-start.5 = (f32[1024,512]{1,0:T(8,128)S(1)}, f32[1024,512]{1,0:T(8,128)}, u32[]{:S(2)}) copy-start(f32[1024,512]{1,0:T(8,128)} %get-tuple-element.300) | copy-start | bytes 6291460 | tf_op jit(solution)/shard_map/while
  181.1 2.0 copy-start.3
  184.5 4.2 %copy-start.1 = (f32[1024,512]{1,0:T(8,128)S(1)}, f32[1024,512]{1,0:T(8,128)}, u32[]{:S(2)}) copy-start(f32[1024,512]{1,0:T(8,128)} %get-tuple-element.322) | copy-start | bytes 6291460 | tf_op jit(solution)/shard_map/while
  184.5 4.2 %copy-start.5 = (f32[1024,512]{1,0:T(8,128)S(1)}, f32[1024,512]{1,0:T(8,128)}, u32[]{:S(2)}) copy-start(f32[1024,512]{1,0:T(8,128)} %get-tuple-element.300) | copy-start | bytes 6291460 | tf_op jit(solution)/shard_map/while
  194.5 2.0 copy-start.3
  197.9 4.2 %copy-start.1 = (f32[1024,512]{1,0:T(8,128)S(1)}, f32[1024,512]{1,0:T(8,128)}, u32[]{:S(2)}) copy-start(f32[1024,512]{1,0:T(8,128)} %get-tuple-element.322) | copy-start | bytes 6291460 | tf_op jit(solution)/shard_map/while
  198.0 4.2 %copy-start.5 = (f32[1024,512]{1,0:T(8,128)S(1)}, f32[1024,512]{1,0:T(8,128)}, u32[]{:S(2)}) copy-start(f32[1024,512]{1,0:T(8,128)} %get-tuple-element.300) | copy-start | bytes 6291460 | tf_op jit(solution)/shard_map/while
  208.0 2.0 copy-start.3
  211.4 4.2 %copy-start.1 = (f32[1024,512]{1,0:T(8,128)S(1)}, f32[1024,512]{1,0:T(8,128)}, u32[]{:S(2)}) copy-start(f32[1024,512]{1,0:T(8,128)} %get-tuple-element.322) | copy-start | bytes 6291460 | tf_op jit(solution)/shard_map/while
  211.4 4.2 %copy-start.5 = (f32[1024,512]{1,0:T(8,128)S(1)}, f32[1024,512]{1,0:T(8,128)}, u32[]{:S(2)}) copy-start(f32[1024,512]{1,0:T(8,128)} %get-tuple-element.300) | copy-start | bytes 6291460 | tf_op jit(solution)/shard_map/while
  221.4 2.0 copy-start.3
  224.8 4.2 %copy-start.1 = (f32[1024,512]{1,0:T(8,128)S(1)}, f32[1024,512]{1,0:T(8,128)}, u32[]{:S(2)}) copy-start(f32[1024,512]{1,0:T(8,128)} %get-tuple-element.322) | copy-start | bytes 6291460 | tf_op jit(solution)/shard_map/while
  224.8 4.2 %copy-start.5 = (f32[1024,512]{1,0:T(8,128)S(1)}, f32[1024,512]{1,0:T(8,128)}, u32[]{:S(2)}) copy-start(f32[1024,512]{1,0:T(8,128)} %get-tuple-element.300) | copy-start | bytes 6291460 | tf_op jit(solution)/shard_map/while
  234.9 2.0 copy-start.3
  238.3 4.2 %copy-start.1 = (f32[1024,512]{1,0:T(8,128)S(1)}, f32[1024,512]{1,0:T(8,128)}, u32[]{:S(2)}) copy-start(f32[1024,512]{1,0:T(8,128)} %get-tuple-element.322) | copy-start | bytes 6291460 | tf_op jit(solution)/shard_map/while
  238.3 4.2 %copy-start.5 = (f32[1024,512]{1,0:T(8,128)S(1)}, f32[1024,512]{1,0:T(8,128)}, u32[]{:S(2)}) copy-start(f32[1024,512]{1,0:T(8,128)} %get-tuple-element.300) | copy-start | bytes 6291460 | tf_op jit(solution)/shard_map/while
  248.3 2.0 copy-start.3
  251.7 4.2 %copy-start.1 = (f32[1024,512]{1,0:T(8,128)S(1)}, f32[1024,512]{1,0:T(8,128)}, u32[]{:S(2)}) copy-start(f32[1024,512]{1,0:T(8,128)} %get-tuple-element.322) | copy-start | bytes 6291460 | tf_op jit(solution)/shard_map/while
  251.7 4.2 %copy-start.5 = (f32[1024,512]{1,0:T(8,128)S(1)}, f32[1024,512]{1,0:T(8,128)}, u32[]{:S(2)}) copy-start(f32[1024,512]{1,0:T(8,128)} %get-tuple-element.300) | copy-start | bytes 6291460 | tf_op jit(solution)/shard_map/while
  265.2 4.2 %copy-start.1 = (f32[1024,512]{1,0:T(8,128)S(1)}, f32[1024,512]{1,0:T(8,128)}, u32[]{:S(2)}) copy-start(f32[1024,512]{1,0:T(8,128)} %get-tuple-element.322) | copy-start | bytes 6291460 | tf_op jit(solution)/shard_map/while
  265.2 4.2 %copy-start.5 = (f32[1024,512]{1,0:T(8,128)S(1)}, f32[1024,512]{1,0:T(8,128)}, u32[]{:S(2)}) copy-start(f32[1024,512]{1,0:T(8,128)} %get-tuple-element.300) | copy-start | bytes 6291460 | tf_op jit(solution)/shard_map/while
  275.2 2.0 copy-start.3
  278.6 4.2 %copy-start.1 = (f32[1024,512]{1,0:T(8,128)S(1)}, f32[1024,512]{1,0:T(8,128)}, u32[]{:S(2)}) copy-start(f32[1024,512]{1,0:T(8,128)} %get-tuple-element.322) | copy-start | bytes 6291460 | tf_op jit(solution)/shard_map/while
  278.6 4.2 %copy-start.5 = (f32[1024,512]{1,0:T(8,128)S(1)}, f32[1024,512]{1,0:T(8,128)}, u32[]{:S(2)}) copy-start(f32[1024,512]{1,0:T(8,128)} %get-tuple-element.300) | copy-start | bytes 6291460 | tf_op jit(solution)/shard_map/while
  288.7 2.0 copy-start.3
  (36 other events, 55.9 us)
Sparse Core Ops, SparseCore 0:
  49.7 25.3 all-gather.1
where the time goes:
time: 355 us; the launch traced here: 353 us
  other arithmetic  137 us (39%)
  blocking collectives  94.5 us (27%)
  local copies, waits for them, and re-layouts  44.7 us (13%)
  matrix products  32 us (9%)
  waiting for transfers between devices  19.8 us (6%)
  between operations  14.2 us (4%)
  loops' own time  11.1 us (3%)
    another operation x32, other arithmetic, advance(): stacked = jnp.stack(term_list)  132 us
    psum x4, blocking collectives, by_axis(): value = lax.psum(value, axis)  55.8 us
    dot_general x16, matrix products, advance(): jnp.einsum('grc,cm->grm', stacked, filtered_cols, preferred_element_type=...  30.6 us
    while x176, local copies, waits for them, and re-layouts  27.1 us
    all_to_all x1, blocking collectives, summed_on_arrival(): parts = lax.all_to_all(split_up(value, dim, length), axis, 0, 0, tiled=True)  24.9 us
    all_gather x1, waiting for transfers between devices, broadcast(): lax.all_gather(value, axis)  19.7 us
    all_to_all x1, blocking collectives, from_everyone(): lax.all_to_all(jnp.broadcast_to(value[None], (length, *value.shape)), axi...  13.7 us
    another operation x1, loops' own time, per_device(): lax.scan(advance, (previous, current), jnp.arange(L // GROUP, dtype=jnp.i...  11.1 us
  transfers between devices with their start and end apart: 1, of which 1 were waited for; matrix products, arithmetic and copies ran while one was open for 2% of the time, Pallas kernels for 0%

commit v1 on v0

v1 whole, which is shorter than its diff:
```python
import functools

import jax
import jax.numpy as jnp
import numpy as np
from jax import lax
from jax.experimental import pallas as pl
from jax.experimental.pallas import tpu as pltpu
from jax.sharding import Mesh
from jax.sharding import PartitionSpec as P

NPIX = 8192
MAPS = 192
L = 64
LMIN = 2
TOP = LMIN + L - 1
NR, NC = 8, 16
CHUNK = NPIX // NC
PIECE = CHUNK // NR
LANES = 256
ROWS = 32
COLS = 256
PROW = ("prow_0", "prow_1")
PCOL = ("pcol_0", "pcol_1")
ALL = PROW + PCOL
bf16, f32 = jnp.bfloat16, jnp.float32


def half_of(r, c):
    if c // 2 == r:
        return 1 - c % 2
    return c % 2 if c // 2 > r else 1 - c % 2


HALF = np.array([[half_of(r, c) for c in range(NC)] for r in range(NR)])
MEMBERS = [[[c for c in range(NC) if HALF[r, c] == s] for s in range(2)] for r in range(NR)]
PIECE_OF = np.array(
    [[8 * HALF[r, c] + MEMBERS[r][HALF[r, c]].index(c) for c in range(NC)] for r in range(NR)]
)
ROW_GROUPS = [[r * NC + c for c in MEMBERS[r][s]] for r in range(NR) for s in range(2)]
TO_COLUMNS = [
    (r * NC + MEMBERS[r][s][j], j * NC + 2 * r + s)
    for r in range(NR) for s in range(2) for j in range(NR)
]
OTHER_HALF = [
    (r * NC + MEMBERS[r][s][j], r * NC + MEMBERS[r][1 - s][j])
    for r in range(NR) for s in range(2) for j in range(NR)
]


def tile_tables():
    plans = []
    for s in range(2):
        plans.append(
            [(512 * s + 32 * u, 32 * u, h, 1) for h in range(2) for u in range(16)]
        )
    for own in range(2):
        other = 1 - own
        mine, theirs = 512 * own, 512 * other
        tiles = [(mine + 32 * u, 512 + 32 * u, 0, 0) for u in range(8)]
        tiles += [(mine + 32 * u, 512 + 32 * u, 1, 1) for u in range(8)]
        tiles += [(mine + 256 + 32 * u, 768 + 32 * u, 1, 0) for u in range(8)]
        if own == 0:
            tiles += [(theirs + 32 * u, 32 * u, h, 1) for h in range(2) for u in range(8)]
        else:
            tiles += [(theirs + 32 * u, 32 * u, 1, 1) for u in range(16)]
        plans.append(tiles)
    most = max(map(len, plans)) + 2
    table = np.zeros((4, most, 4), np.int32)
    counts = np.zeros((4,), np.int32)
    for kind, tiles in enumerate(plans):
        counts[kind] = len(tiles)
        table[kind] = np.array(tiles + [tiles[-1]] * (most - len(tiles)))
    return table, counts


TABLE, COUNTS = tile_tables()


def basis_matrix():
    g = [1.0]
    for k in range(1, TOP + 1):
        g.append(g[-1] * (2 * k - 1) / (2 * k))
    matrix = np.zeros((L, TOP + 1))
    for row in range(L):
        degree = row + LMIN
        for k in range(degree + 1):
            matrix[row, abs(degree - 2 * k)] += g[k] * g[degree - k]
        matrix[row] *= 2.0 * (2.0 * degree + 1.0) / NPIX
    return np.repeat(matrix, 8, axis=1).astype(np.float32)


BASIS = basis_matrix()


def partial_kernel(order_ref, cov_ref, maps_ref, out_ref):
    product = jnp.dot(cov_ref[...], maps_ref[...], preferred_element_type=f32)
    for piece in range(NC):
        rows = product[PIECE * piece : PIECE * (piece + 1)]
        out_ref[order_ref[piece]] = rows.astype(bf16)


def spectra_kernel(
    kind_ref, counts_ref, table_ref, cos_ref, rows_ref, cols_ref, basis_ref, out_ref,
    maps, weights, even, odd, total,
):
    kind = kind_ref[0]
    zeros = jnp.zeros((CHUNK, LANES - MAPS), bf16)
    col_maps = jnp.concatenate([cols_ref[...], zeros], axis=1)
    row_maps = jnp.concatenate([rows_ref[...], zeros], axis=1)
    weights[0] = col_maps[:COLS]
    weights[1] = col_maps[COLS:]
    maps[:CHUNK] = row_maps
    maps[CHUNK:] = col_maps
    row_sum = jnp.sum(row_maps.astype(f32), axis=0, keepdims=True)
    col_sum = jnp.sum(col_maps.astype(f32), axis=0, keepdims=True)
    diagonal = kind >= 2
    alpha = jnp.where(diagonal, 0.5, 1.0)
    beta = jnp.where(diagonal, 0.5, 0.0)
    total[...] = jnp.zeros_like(total)
    total[0, 0:1] = col_sum * (alpha * row_sum + beta * col_sum)

    def generate(t, slot):
        row = pl.multiple_of(table_ref[kind, t, 0], ROWS)
        col = pl.multiple_of(table_ref[kind, t, 2] * COLS, COLS)
        x = cos_ref[pl.ds(row, ROWS), pl.ds(col, COLS)]
        twice = x + x
        previous, current = jnp.ones_like(x), x
        slot[0] = x.astype(bf16)
        for k in range(2, TOP + 1):
            previous, current = current, twice * current - previous
            slot[k - 1] = current.astype(bf16)

    def contract(t, slot):
        row = pl.multiple_of(table_ref[kind, t, 1], ROWS)
        weight = jnp.where(table_ref[kind, t, 3] == 1, 1.0, 0.5)
        left = maps[pl.ds(row, ROWS)].astype(f32) * weight
        right = weights[table_ref[kind, t, 2]]
        image = jnp.dot(slot[...].reshape(TOP * ROWS, COLS), right, preferred_element_type=f32)
        for k in range(TOP):
            product = image[ROWS * k : ROWS * (k + 1)] * left
            total[k + 1] += jnp.sum(product.reshape(ROWS // 8, 8, LANES), axis=0)

    generate(0, even)

    def step(pair, carry):
        t = 2 * pair
        generate(t + 1, odd)
        contract(t, even)
        generate(t + 2, even)
        contract(t + 1, odd)
        return carry

    lax.fori_loop(0, counts_ref[kind] // 2, step, 0)
    sums = total[...].reshape((TOP + 1) * 8, LANES)
    out_ref[...] = jnp.dot(
        basis_ref[...], sums, preferred_element_type=f32, precision=lax.Precision.HIGHEST
    )


SMEM = pl.BlockSpec(memory_space=pltpu.SMEM)
VMEM = pl.BlockSpec(memory_space=pltpu.VMEM)


def partial_products(order, cov, maps):
    return pl.pallas_call(
        partial_kernel,
        out_shape=jax.ShapeDtypeStruct((NC, PIECE, MAPS), bf16),
        in_specs=[SMEM, VMEM, VMEM],
        out_specs=VMEM,
        name="partial",
    )(order, cov, maps)


def block_spectra(kind, cosines, rows, cols):
    return pl.pallas_call(
        spectra_kernel,
        out_shape=jax.ShapeDtypeStruct((L, LANES), f32),
        in_specs=[SMEM, SMEM, SMEM, VMEM, VMEM, VMEM, VMEM],
        out_specs=VMEM,
        scratch_shapes=[
            pltpu.VMEM((2 * CHUNK, LANES), bf16),
            pltpu.VMEM((2, COLS, LANES), bf16),
            pltpu.VMEM((TOP, ROWS, COLS), bf16),
            pltpu.VMEM((TOP, ROWS, COLS), bf16),
            pltpu.VMEM((TOP + 1, 8, LANES), f32),
        ],
        cost_estimate=pl.CostEstimate(flops=9 * 10**9, bytes_accessed=4 * 10**6, transcendentals=0),
        name="spectra",
    )(kind, jnp.asarray(COUNTS), jnp.asarray(TABLE), cosines, rows, cols, jnp.asarray(BASIS))


def from_everyone(value, axis, groups=None):
    length = NR
    copies = jnp.broadcast_to(value[None], (length, *value.shape))
    return lax.all_to_all(copies, axis, 0, 0, axis_index_groups=groups, tiled=True)


def everywhere(value):
    value = value + lax.ppermute(value, PROW[1], [(0, 1), (1, 0)])
    for axis in (PROW[0],) + PCOL:
        value = value + lax.ppermute(value, axis, [(0, 1), (1, 0), (2, 3), (3, 2)])
        value = value + lax.ppermute(value, axis, [(0, 3), (3, 0), (2, 1), (1, 2)])
    return value


def per_device(inverse_cov, cosines, sky_maps):
    r, c = lax.axis_index(PROW), lax.axis_index(PCOL)
    half = jnp.asarray(HALF, jnp.int32)[r, c]
    places = np.zeros((NR, NC), np.int32)
    for row in range(NR):
        places[row, PIECE_OF[row]] = np.arange(NC)
    order = jnp.asarray(places)[r]
    kind = jnp.where(c // 2 == r, 2 + c % 2, half).astype(jnp.int32).reshape(1)

    partial = partial_products(order, inverse_cov, sky_maps)
    parts = lax.all_to_all(partial, PCOL, 0, 0, tiled=True)
    piece = jnp.sum(parts.astype(f32), axis=0).astype(bf16)

    moved = lax.ppermute(piece, ALL, TO_COLUMNS)
    rows = from_everyone(piece, ALL, ROW_GROUPS).reshape(CHUNK, MAPS)
    other = lax.ppermute(rows, ALL, OTHER_HALF)
    cols = from_everyone(moved, PROW).reshape(CHUNK, MAPS)

    share = block_spectra(kind, cosines, rows, cols)
    spectra = everywhere(share[:, :MAPS])
    first = jnp.where(half == 0, rows, other)
    second = jnp.where(half == 0, other, rows)
    return jnp.concatenate([first, second], axis=0), spectra


def solution(mesh):
    split = Mesh(mesh.devices.reshape(4, 2, 4, 4), ALL)
    placed = (P(PROW, PCOL), P(PROW, PCOL), P(PCOL, None))
    return jax.shard_map(
        per_device, mesh=split, in_specs=placed, out_specs=(P(PROW, None), P()), check_vma=False
    )
```

time: 355 us -> 107 us (0.30)
  other arithmetic: 137 us -> 2.71 us
  blocking collectives: 94.5 us -> 19.5 us
  local copies, waits for them, and re-layouts: 44.7 us -> 7.37 us
  matrix products: 32 us -> 0 us
  Pallas kernels: 0 us -> 23 us
  waiting for transfers between devices: 19.8 us -> 38.7 us
  starting transfers between devices: 0.04 us -> 12.6 us
  between operations: 14.2 us -> 2.01 us
  loops' own time: 11.1 us -> 0 us
    another operation x48 -> x0, other arithmetic: 134 us -> none  [the longest x32 132 us: advance(): stacked = jnp.stack(term_list)]
    psum x4 -> x0, blocking collectives: 55.8 us -> none  [by_axis(): value = lax.psum(value, axis)]
    dot_general x17 -> x0, matrix products: 32 us -> none  [the longest x16 30.6 us: advance(): jnp.einsum('grc,cm->grm', stacked, filtered_cols, preferred_element_type=...]
    ppermute x0 -> x9, waiting for transfers between devices: none -> 28.6 us  [the longest x3 12.2 us: everywhere(): value = value + lax.ppermute(value, axis, [(0, 3), (3, 0), (2, 1), (1, 2)])]
    while x176 -> x0, local copies, waits for them, and re-layouts: 27.1 us -> none
    pallas_call x0 -> x2, Pallas kernels: none -> 23 us  [the longest x1 20.5 us: block_spectra(): pl.pallas_call(spectra_kernel, out_shape=jax.ShapeDtypeStruct((L, LANES),...]
    all_gather x1 -> x0, waiting for transfers between devices: 19.7 us -> none  [broadcast(): lax.all_gather(value, axis)]
    all_to_all x2 -> x1, blocking collectives: 38.7 us -> 19.5 us  [per_device(): parts = lax.all_to_all(partial, PCOL, 0, 0, tiled=True)]
  transfers between devices with their start and end apart: 1 -> 11, of which waited for: 1 -> 10; matrix products, arithmetic and copies ran while one was open for 2% -> 3% of each run, Pallas kernels for 0% -> 0%
where the time goes in v1:
time: 107 us; the launch traced here: 106 us
  waiting for transfers between devices  38.7 us (36%)
  Pallas kernels  23 us (21%)
  blocking collectives  19.5 us (18%)
  starting transfers between devices  12.6 us (12%)
  local copies, waits for them, and re-layouts  7.37 us (7%)
  other arithmetic  2.71 us (3%)
  between operations  2.01 us (2%)
    pallas_call x1, Pallas kernels, block_spectra(): pl.pallas_call(spectra_kernel, out_shape=jax.ShapeDtypeStruct((L, LANES),...  20.5 us
    all_to_all x1, blocking collectives, per_device(): parts = lax.all_to_all(partial, PCOL, 0, 0, tiled=True)  19.5 us
    ppermute x3, waiting for transfers between devices, everywhere(): value = value + lax.ppermute(value, axis, [(0, 3), (3, 0), (2, 1), (1, 2)])  12.2 us
    ppermute x3, waiting for transfers between devices, everywhere(): value = value + lax.ppermute(value, axis, [(0, 1), (1, 0), (2, 3), (3, 2)])  11.7 us
    all_to_all x2, waiting for transfers between devices, from_everyone(): lax.all_to_all(copies, axis, 0, 0, axis_index_groups=groups, tiled=True)  10.1 us
    all_to_all x2, starting transfers between devices, from_everyone(): lax.all_to_all(copies, axis, 0, 0, axis_index_groups=groups, tiled=True)  8.74 us
    unnamed x6, local copies, waits for them, and re-layouts  3.4 us
    ppermute x1, waiting for transfers between devices, per_device(): moved = lax.ppermute(piece, ALL, TO_COLUMNS)  3.35 us
  transfers between devices with their start and end apart: 11, of which 10 were waited for; matrix products, arithmetic and copies ran while one was open for 3% of the time, Pallas kernels for 0%

profile of v1, /device:TPU:0, one launch (start us, length us, event | category | flops | bytes accessed | tf_op | source)
XLA Modules:
  0.0 106.0 jit_solution(15089244000094826238)
XLA Ops:
  0.6 1.8 %copy.10.maps_ref = bf16[512,192]{1,0:T(8,128)(2,1)} copy(bf16[512,192]{0,1:T(8,128)(2,1)} %param.10) | data formatting | bytes 393216 | tf_op args[2]
  2.4 1.2 %dynamic-slice_bitcast_fusion.order_ref = s32[16]{0:T(128)} fusion(s32[8,16]{1,0:T(8,128)} %constant.62.clone, s32[]{:T(128)S(6)} %select_n.33), kind=kLoop, calls=%fused_computation.3 | loop fusion | bytes 132 | tf_op jit(solution)/shard_map/squeeze | solution.py:213
  3.6 2.5 %partial.1 = bf16[16,64,192]{2,1,0:T(8,128)(2,1)} custom-call(s32[16]{0:T(128)} %dynamic-slice_bitcast_fusion.order_ref, bf16[1024,512]{1,0:T(8,128)(2,1)} %cov_ref.1, bf16[512,192]{1,0:T(8,128)(2,1)} %copy.10.maps_ref), custom_call_target="tpu_custom_call" | custom-call | tf_op jit(solution)/shard_map/partial/pallas_call | solution.py:166
  6.1 19.5 %all_to_all.15 = bf16[16,64,192]{2,1,0:T(8,128)(2,1)S(1)} all-to-all(bf16[16,64,192]{2,1,0:T(8,128)(2,1)} %partial.1), channel_id=1, replica_groups=mesh['prow_0'=4,'prow_1'=2,'pcol_0'=4,'pcol_1'=4] {'pcol_0','pcol_1'}, dimensions={0} | all-to-all | bytes 786432 | tf_op jit(solution)/shard_map/all_to_all | solution.py:217
  25.6 0.1 reduce_sum.12
  25.7 0.7 broadcast_in_dim.4
  26.5 3.4 %all-to-all-start.1 = ((bf16[8,64,192]{2,1,0:T(8,128)(2,1)}), bf16[8,64,192]{2,1,0:T(8,128)(2,1)S(1)}, u32[]{:S(2)}, u32[]{:S(2)}) async-start(bf16[8,64,192]{2,1,0:T(8,128)(2,1)} %broadcast_in_dim.4), calls=%async_computation.1 | async-start | bytes 524288 | tf_op jit(solution)/shard_map/all_to_all | solution.py:196
  29.9 0.6 collective-permute-start.1
  30.5 3.3 %collective-permute-done.1 = bf16[64,192]{1,0:T(8,128)(2,1)S(1)} collective-permute-done((bf16[64,192]{1,0:T(8,128)(2,1)S(1)}, bf16[64,192]{1,0:T(8,128)(2,1)S(1)}, u32[]{:S(2)}, u32[]{:S(2)}) %collective-permute-start.1) | collective-permute-done | bytes 24608 | tf_op jit(solution)/shard_map/ppermute | solution.py:220
  33.9 4.5 %all-to-all-done.1 = bf16[8,64,192]{2,1,0:T(8,128)(2,1)S(1)} async-done(((bf16[8,64,192]{2,1,0:T(8,128)(2,1)}), bf16[8,64,192]{2,1,0:T(8,128)(2,1)S(1)}, u32[]{:S(2)}, u32[]{:S(2)}) %all-to-all-start.1) | async-done | bytes 196640 | tf_op jit(solution)/shard_map/all_to_all | solution.py:196
  38.4 0.0 copy-start
  38.4 0.8 broadcast_in_dim.5
  39.2 5.3 %all-to-all-start.2 = ((bf16[8,64,192]{2,1,0:T(8,128)(2,1)}), bf16[8,64,192]{2,1,0:T(8,128)(2,1)S(1)}, u32[]{:S(2)}, u32[]{:S(2)}) async-start(bf16[8,64,192]{2,1,0:T(8,128)(2,1)} %broadcast_in_dim.5), calls=%async_computation.2 | async-start | bytes 524288 | tf_op jit(solution)/shard_map/all_to_all | solution.py:196
  44.5 1.3 %dynamic_slice.6 = s32[1,1]{1,0:T(1,128)} dynamic-slice(s32[8,16]{1,0:T(8,128)} %constant.61.clone, s32[]{:T(128)S(6)} %select_n.33, s32[]{:T(128)S(6)} %select_n.34), dynamic_slice_sizes={1,1} | dynamic-slice | bytes 12 | tf_op jit(solution)/shard_map/dynamic_slice | solution.py:209
  46.4 5.6 %all-to-all-done.2 = bf16[8,64,192]{2,1,0:T(8,128)(2,1)S(1)} async-done(((bf16[8,64,192]{2,1,0:T(8,128)(2,1)}), bf16[8,64,192]{2,1,0:T(8,128)(2,1)S(1)}, u32[]{:S(2)}, u32[]{:S(2)}) %all-to-all-start.2) | async-done | bytes 196640 | tf_op jit(solution)/shard_map/all_to_all | solution.py:196
  52.0 0.0 copy-start.1
  52.0 0.0 copy-done
  52.0 0.7 copy-done.1
  52.7 20.5 %spectra.1 = f32[64,256]{1,0:T(8,128)} custom-call(s32[1]{0:T(128)} %bitcast.3.kind_ref, s32[4]{0:T(128)} %constant.63.clone.counts_ref, s32[4,42,4]{2,1,0:T(8,128)} %constant.64.clone.table_ref, f32[1024,512]{1,0:T(8,128)} %cos_ref.1, bf16[512,192]{1,0:T(8,128)(2,1)} %bitcast.9, bf16[512,192]{1,0:T(8,128)(2,1)} %bitcast.11, f32[64,528]{1,0:T(8,128)} %constant.65.clone.basis_ref), custom_call_target="tpu_custom_call" | custom-call | flops 8999999488 | bytes 4000000 | tf_op jit(solution)/shard_map/spectra/pallas_call | solution.py:176
  73.2 0.0 collective-permute-start.2
  73.2 1.5 %collective-permute-done.2 = f32[64,192]{1,0:T(8,128)S(1)} collective-permute-done((f32[64,192]{1,0:T(8,128)}, f32[64,192]{1,0:T(8,128)S(1)}, u32[]{:S(2)}, u32[]{:S(2)}) %collective-permute-start.2) | collective-permute-done | bytes 49184 | tf_op jit(solution)/shard_map/ppermute | solution.py:200
  74.7 0.9 slice_add_fusion
  75.5 0.1 collective-permute-start.3
  75.6 0.1 collective-permute-start
  75.7 4.2 %collective-permute-done.3 = f32[64,192]{1,0:T(8,128)S(1)} collective-permute-done((f32[64,192]{1,0:T(8,128)S(1)}, f32[64,192]{1,0:T(8,128)S(1)}, u32[]{:S(2)}, u32[]{:S(2)}) %collective-permute-start.3) | collective-permute-done | bytes 49184 | tf_op jit(solution)/shard_map/ppermute | solution.py:202
  79.9 0.1 collective-permute-start.4
  80.0 5.5 %collective-permute-done.4 = f32[64,192]{1,0:T(8,128)S(1)} collective-permute-done((f32[64,192]{1,0:T(8,128)S(1)}, f32[64,192]{1,0:T(8,128)S(1)}, u32[]{:S(2)}, u32[]{:S(2)}) %collective-permute-start.4) | collective-permute-done | bytes 49184 | tf_op jit(solution)/shard_map/ppermute | solution.py:203
  85.5 0.1 collective-permute-start.5
  85.6 4.3 %collective-permute-done.5 = f32[64,192]{1,0:T(8,128)S(1)} collective-permute-done((f32[64,192]{1,0:T(8,128)S(1)}, f32[64,192]{1,0:T(8,128)S(1)}, u32[]{:S(2)}, u32[]{:S(2)}) %collective-permute-start.5) | collective-permute-done | bytes 49184 | tf_op jit(solution)/shard_map/ppermute | solution.py:202
  89.8 0.1 collective-permute-start.6
  90.6 4.8 %collective-permute-done.6 = f32[64,192]{1,0:T(8,128)S(1)} collective-permute-done((f32[64,192]{1,0:T(8,128)S(1)}, f32[64,192]{1,0:T(8,128)S(1)}, u32[]{:S(2)}, u32[]{:S(2)}) %collective-permute-start.6) | collective-permute-done | bytes 49184 | tf_op jit(solution)/shard_map/ppermute | solution.py:203
  95.4 0.1 collective-permute-start.7
  95.5 0.0 collective-permute-done
  95.5 1.0 broadcast_select_fusion.1
  96.5 3.2 %collective-permute-done.7 = f32[64,192]{1,0:T(8,128)S(1)} collective-permute-done((f32[64,192]{1,0:T(8,128)S(1)}, f32[64,192]{1,0:T(8,128)S(1)}, u32[]{:S(2)}, u32[]{:S(2)}) %collective-permute-start.7) | collective-permute-done | bytes 49184 | tf_op jit(solution)/shard_map/ppermute | solution.py:202
  99.8 2.7 %collective-permute-start.8 = (f32[64,192]{1,0:T(8,128)S(1)}, f32[64,192]{1,0:T(8,128)S(1)}, u32[]{:S(2)}, u32[]{:S(2)}) collective-permute-start(f32[64,192]{1,0:T(8,128)S(1)} %add.53), channel_id=1, source_target_pairs={{0,3},{3,0},{2,1},{1,2},{4,7},{7,4},{6,5},{5,6},{8,11},{11,8},{10,... | collective-permute-start | bytes 147464 | tf_op jit(solution)/shard_map/ppermute | solution.py:203
  102.4 0.1 pad_maximum_fusion
  102.5 0.9 copy.11
  103.5 1.9 %collective-permute-done.8 = f32[64,192]{1,0:T(8,128)S(1)} collective-permute-done((f32[64,192]{1,0:T(8,128)S(1)}, f32[64,192]{1,0:T(8,128)S(1)}, u32[]{:S(2)}, u32[]{:S(2)}) %collective-permute-start.8) | collective-permute-done | bytes 49184 | tf_op jit(solution)/shard_map/ppermute | solution.py:203
  105.3 0.6 add.54
  (5 shorter events, 0.0 us)
Async XLA Ops:
  26.5 11.9 %all-to-all-start.1 = ((bf16[8,64,192]{2,1,0:T(8,128)(2,1)}), bf16[8,64,192]{2,1,0:T(8,128)(2,1)S(1)}, u32[]{:S(2)}, u32[]{:S(2)}) async-start(bf16[8,64,192]{2,1,0:T(8,128)(2,1)} %broadcast_in_dim.4), calls=%async_computation.1 | async-start | bytes 524288 | tf_op jit(solution)/shard_map/all_to_all | solution.py:196
  29.9 4.0 %collective-permute-start.1 = (bf16[64,192]{1,0:T(8,128)(2,1)S(1)}, bf16[64,192]{1,0:T(8,128)(2,1)S(1)}, u32[]{:S(2)}, u32[]{:S(2)}) collective-permute-start(bf16[64,192]{1,0:T(8,128)(2,1)S(1)} %reduce_sum.12), channel_id=1, source_target_pairs={{1,0},{2,16},{4,32},{6,48},{8,64},{10,80},{12,96},{14,112},{0,1},{... | collective-permute-start | bytes 73736 | tf_op jit(solution)/shard_map/ppermute | solution.py:220
  38.4 13.6 %copy-start = (bf16[8,64,192]{2,1,0:T(8,128)(2,1)}, bf16[8,64,192]{2,1,0:T(8,128)(2,1)S(1)}, u32[]{:S(2)}) copy-start(bf16[8,64,192]{2,1,0:T(8,128)(2,1)S(1)} %all-to-all-done.1) | copy-start | bytes 589828
  39.2 12.8 %all-to-all-start.2 = ((bf16[8,64,192]{2,1,0:T(8,128)(2,1)}), bf16[8,64,192]{2,1,0:T(8,128)(2,1)S(1)}, u32[]{:S(2)}, u32[]{:S(2)}) async-start(bf16[8,64,192]{2,1,0:T(8,128)(2,1)} %broadcast_in_dim.5), calls=%async_computation.2 | async-start | bytes 524288 | tf_op jit(solution)/shard_map/all_to_all | solution.py:196
  52.0 0.7 copy-start.1
  73.2 1.5 %collective-permute-start.2 = (f32[64,192]{1,0:T(8,128)}, f32[64,192]{1,0:T(8,128)S(1)}, u32[]{:S(2)}, u32[]{:S(2)}) collective-permute-start(f32[64,192]{1,0:T(8,128)} %bitcast.12), channel_id=1, source_target_pairs={{0,16},{16,0},{1,17},{17,1},{2,18},{18,2},{3,19},{19,3},{4,20},{20... | collective-permute-start | bytes 147464 | tf_op jit(solution)/shard_map/ppermute | solution.py:200
  75.5 4.3 %collective-permute-start.3 = (f32[64,192]{1,0:T(8,128)S(1)}, f32[64,192]{1,0:T(8,128)S(1)}, u32[]{:S(2)}, u32[]{:S(2)}) collective-permute-start(f32[64,192]{1,0:T(8,128)S(1)} %slice_add_fusion), channel_id=1, source_target_pairs={{0,32},{32,0},{64,96},{96,64},{1,33},{33,1},{65,97},{97,65},{2,34}... | collective-permute-start | bytes 147464 | tf_op jit(solution)/shard_map/ppermute | solution.py:202
  75.6 19.9 %collective-permute-start = (bf16[512,192]{1,0:T(8,128)(2,1)}, bf16[512,192]{1,0:T(8,128)(2,1)S(1)}, u32[]{:S(2)}, u32[]{:S(2)}) collective-permute-start(bf16[512,192]{1,0:T(8,128)(2,1)} %bitcast.10), channel_id=1, source_target_pairs={{1,0},{2,3},{4,5},{6,7},{8,9},{10,11},{12,13},{14,15},{0,1},{3,2},... | collective-permute-start | bytes 589832 | tf_op jit(solution)/shard_map/ppermute | solution.py:222
  79.9 5.6 %collective-permute-start.4 = (f32[64,192]{1,0:T(8,128)S(1)}, f32[64,192]{1,0:T(8,128)S(1)}, u32[]{:S(2)}, u32[]{:S(2)}) collective-permute-start(f32[64,192]{1,0:T(8,128)S(1)} %add.49), channel_id=1, source_target_pairs={{0,96},{96,0},{64,32},{32,64},{1,97},{97,1},{65,33},{33,65},{2,98}... | collective-permute-start | bytes 147464 | tf_op jit(solution)/shard_map/ppermute | solution.py:203
  85.5 4.3 %collective-permute-start.5 = (f32[64,192]{1,0:T(8,128)S(1)}, f32[64,192]{1,0:T(8,128)S(1)}, u32[]{:S(2)}, u32[]{:S(2)}) collective-permute-start(f32[64,192]{1,0:T(8,128)S(1)} %add.50), channel_id=1, source_target_pairs={{0,4},{4,0},{8,12},{12,8},{1,5},{5,1},{9,13},{13,9},{2,6},{6,2},{1... | collective-permute-start | bytes 147464 | tf_op jit(solution)/shard_map/ppermute | solution.py:202
  89.8 5.6 %collective-permute-start.6 = (f32[64,192]{1,0:T(8,128)S(1)}, f32[64,192]{1,0:T(8,128)S(1)}, u32[]{:S(2)}, u32[]{:S(2)}) collective-permute-start(f32[64,192]{1,0:T(8,128)S(1)} %add.51), channel_id=1, source_target_pairs={{0,12},{12,0},{8,4},{4,8},{1,13},{13,1},{9,5},{5,9},{2,14},{14,2},... | collective-permute-start | bytes 147464 | tf_op jit(solution)/shard_map/ppermute | solution.py:203
  95.4 4.3 %collective-permute-start.7 = (f32[64,192]{1,0:T(8,128)S(1)}, f32[64,192]{1,0:T(8,128)S(1)}, u32[]{:S(2)}, u32[]{:S(2)}) collective-permute-start(f32[64,192]{1,0:T(8,128)S(1)} %add.52), channel_id=1, source_target_pairs={{0,1},{1,0},{2,3},{3,2},{4,5},{5,4},{6,7},{7,6},{8,9},{9,8},{10,11... | collective-permute-start | bytes 147464 | tf_op jit(solution)/shard_map/ppermute | solution.py:202
  99.8 5.6 %collective-permute-start.8 = (f32[64,192]{1,0:T(8,128)S(1)}, f32[64,192]{1,0:T(8,128)S(1)}, u32[]{:S(2)}, u32[]{:S(2)}) collective-permute-start(f32[64,192]{1,0:T(8,128)S(1)} %add.53), channel_id=1, source_target_pairs={{0,3},{3,0},{2,1},{1,2},{4,7},{7,4},{6,5},{5,6},{8,11},{11,8},{10,... | collective-permute-start | bytes 147464 | tf_op jit(solution)/shard_map/ppermute | solution.py:203

commit v2 on v1

v2 whole, which is shorter than its diff:
```python
import functools

import jax
import jax.numpy as jnp
import numpy as np
from jax import lax
from jax.experimental import pallas as pl
from jax.experimental.pallas import tpu as pltpu
from jax.sharding import Mesh
from jax.sharding import PartitionSpec as P

NPIX = 8192
MAPS = 192
L = 64
LMIN = 2
TOP = LMIN + L - 1
NR, NC = 8, 16
CHUNK = NPIX // NC
PIECE = CHUNK // NR
LANES = 256
ROWS = 32
COLS = 256
LOW = 9
CENTRES = (18, 37, 56)
PROW = ("prow_0", "prow_1")
PCOL = ("pcol_0", "pcol_1")
ALL = PROW + PCOL
bf16, f16, f32 = jnp.bfloat16, jnp.float16, jnp.float32
MASKS = (1, 2, 6)
ORDER = (0, 1, 2, 3, 6, 7, 4, 5)


def half_of(r, c):
    return c % 2 if c // 2 > r else 1 - c % 2


MEMBERS = [
    [[c for c in range(NC) if half_of(r, c) == s] for s in range(2)] for r in range(NR)
]
EACH = [(r, s, g) for r in range(NR) for s in range(2) for g in range(NR)]
TO_COLUMNS = [(r * NC + MEMBERS[r][s][g], g * NC + 2 * r + s) for r, s, g in EACH]
OTHER_HALF = [(r * NC + MEMBERS[r][s][g], r * NC + MEMBERS[r][1 - s][g]) for r, s, g in EACH]
ROW_STEPS = [
    [(r * NC + MEMBERS[r][s][g], r * NC + MEMBERS[r][s][g ^ mask]) for r, s, g in EACH]
    for mask in MASKS
]
COLUMN_STEPS = [
    [(r * NC + c, (r ^ mask) * NC + c) for r in range(NR) for c in range(NC)] for mask in MASKS
]


def basis_matrix():
    g = [1.0]
    for k in range(1, TOP + 1):
        g.append(g[-1] * (2 * k - 1) / (2 * k))
    cheb = np.zeros((L, TOP + 1))
    for row in range(L):
        degree = row + LMIN
        for k in range(degree + 1):
            cheb[row, abs(degree - 2 * k)] += g[k] * g[degree - k]
        cheb[row] *= 2.0 * (2.0 * degree + 1.0) / NPIX
    columns = [cheb[:, k] for k in range(LOW)]
    for n in CENTRES:
        columns.append(cheb[:, n])
        columns += [cheb[:, n - a] + cheb[:, n + a] for a in range(1, LOW + 1)]
        columns += [cheb[:, n - a] - cheb[:, n + a] for a in range(1, LOW + 1)]
    matrix = np.stack(columns, axis=1)
    assert matrix.shape == (L, TOP + 1)
    return np.repeat(matrix, 8, axis=1).astype(np.float32)


BASIS = basis_matrix()


def basis_functions(x):
    y = x + x
    t, u = [jnp.ones_like(x), x], [jnp.ones_like(x), y]
    for k in range(2, LOW + 1):
        t.append(y * t[k - 1] - t[k - 2])
        if k < LOW:
            u.append(y * u[k - 1] - u[k - 2])
    square = 1.0 - x * x
    double = t[9] + t[9]
    t18, u17 = double * t[9] - 1.0, double * u[8]
    v18 = square * u17
    double = t18 + t18
    t36, v36 = double * t18 - 1.0, double * v18
    t37, v37 = t36 * x - v36, v36 * x + t36 * square
    t19, u18 = t18 * x - v18, u17 * x + t18
    v19 = square * u18
    t56, v56 = t37 * t19 - v37 * u18, v37 * t19 + t37 * v19
    low_t = [None] + [value.astype(bf16) for value in t[1:]]
    low_u = [None] + [value.astype(bf16) for value in u[1:]]
    yield from low_t[1:LOW]
    for tn, vn in ((t18, v18), (t37, v37), (t56, v56)):
        tn, vn = tn.astype(bf16), vn.astype(bf16)
        yield tn
        for a in range(1, LOW + 1):
            yield tn * low_t[a]
        yield vn
        for a in range(2, LOW + 1):
            yield vn * low_u[a - 1]


def partial_kernel(place_ref, cov_ref, maps_ref, out_ref):
    r = place_ref[0]
    product = lax.dot_general(
        cov_ref[...], maps_ref[...], (((1,), (1,)), ((), ())), preferred_element_type=f32
    )
    for g in range(NR):
        flip = (r >= g).astype(jnp.int32)
        for s in range(2):
            piece = NR * s + g
            rows = product[PIECE * piece : PIECE * (piece + 1)]
            out_ref[2 * g + jnp.where(flip == 1, 1 - s, s)] = rows


def spectra_kernel(
    place_ref, cos_ref, rows_ref, cols_ref, basis_ref, out_ref, maps, weights, even, odd, total
):
    r, c = place_ref[0], place_ref[1]
    group, own = c // 2, c % 2
    other = 1 - own
    diagonal = group == r
    half = jnp.where(group > r, own, other)
    zeros = jnp.zeros((PIECE, LANES - MAPS), bf16)
    row_sum = col_sum = jnp.zeros((8, LANES), f32)
    for place in range(NR):
        rows = jnp.concatenate([rows_ref[place], zeros], axis=1)
        at = pl.multiple_of((group ^ ORDER[place]) * PIECE, PIECE)
        maps[pl.ds(at, PIECE)] = rows
        cols = jnp.concatenate([cols_ref[place], zeros], axis=1)
        at = pl.multiple_of((r ^ ORDER[place]) * PIECE, PIECE)
        weights[pl.ds(at, PIECE)] = cols
        maps[pl.ds(CHUNK + at, PIECE)] = cols
        row_sum += jnp.sum(rows.astype(f32).reshape(PIECE // 8, 8, LANES), axis=0)
        col_sum += jnp.sum(cols.astype(f32).reshape(PIECE // 8, 8, LANES), axis=0)
    row_sum = jnp.sum(row_sum, axis=0, keepdims=True)
    col_sum = jnp.sum(col_sum, axis=0, keepdims=True)
    alpha = jnp.where(diagonal, 0.5, 1.0)
    beta = jnp.where(diagonal, 0.5, 0.0)
    total[...] = jnp.zeros_like(total)
    total[0, 0:1] = col_sum * (alpha * row_sum + beta * col_sum)

    def tile(t):
        part, first = t // 8, 32 * (t % 8)
        plain_row = 32 * (t % 16)
        plain = (CHUNK * half + plain_row, plain_row, t // 16, 1.0)
        mine = part < 3
        low = jnp.logical_or(part == 2, jnp.logical_and(part == 4, own == 1))
        row = first + jnp.where(low, 256, 0)
        column = jnp.where(mine, jnp.minimum(part, 1), jnp.where(part == 3, own, 1))
        weight = jnp.where(jnp.logical_or(part == 0, part == 2), 0.5, 1.0)
        chosen = (
            CHUNK * jnp.where(mine, own, other) + row,
            CHUNK * jnp.where(mine, 1, 0) + row,
            column,
            weight,
        )
        return [jnp.where(diagonal, a, b) for a, b in zip(chosen, plain)]

    def generate(t, slot):
        cos_row, _, column, _ = tile(t)
        cos_row = pl.multiple_of(cos_row, ROWS)
        column = pl.multiple_of(column * COLS, COLS)
        for first in range(0, ROWS, 16):
            x = cos_ref[pl.ds(cos_row + first, 16), pl.ds(column, COLS)]
            for k, value in enumerate(basis_functions(x)):
                slot[k, first : first + 16] = value

    def contract(t, slot):
        _, map_row, column, weight = tile(t)
        left = maps[pl.ds(pl.multiple_of(map_row, ROWS), ROWS)].astype(f32) * weight
        right = weights[pl.ds(pl.multiple_of(column * COLS, COLS), COLS)]
        image = jnp.dot(slot[...].reshape(TOP * ROWS, COLS), right, preferred_element_type=f32)
        for k in range(TOP):
            product = image[ROWS * k : ROWS * (k + 1)] * left
            total[k + 1] += jnp.sum(product.reshape(ROWS // 8, 8, LANES), axis=0)

    count = jnp.where(diagonal, 40, 32)
    generate(0, even)

    def step(pair, carry):
        t = 2 * pair
        generate(t + 1, odd)
        contract(t, even)
        generate(jnp.minimum(t + 2, count - 1), even)
        contract(t + 1, odd)
        return carry

    lax.fori_loop(0, count // 2, step, 0)
    sums = total[...].reshape((TOP + 1) * 8, LANES)
    spectra = jnp.dot(
        basis_ref[...], sums, preferred_element_type=f32, precision=lax.Precision.HIGHEST
    )
    out_ref[...] = spectra[:, :MAPS]


def assemble_kernel(place_ref, rows_ref, other_ref, out_ref, scratch):
    r, c = place_ref[0], place_ref[1]
    group = c // 2
    half = jnp.where(group > r, c % 2, 1 - c % 2)
    for place in range(NR):
        at = (group ^ ORDER[place]) * PIECE
        scratch[pl.ds(pl.multiple_of(CHUNK * half + at, PIECE), PIECE)] = rows_ref[place]
        scratch[pl.ds(pl.multiple_of(CHUNK * (1 - half) + at, PIECE), PIECE)] = other_ref[place]
    out_ref[...] = scratch[...].T


SMEM = pl.BlockSpec(memory_space=pltpu.SMEM)
VMEM = pl.BlockSpec(memory_space=pltpu.VMEM)


def partial_products(place, cov, maps):
    return pl.pallas_call(
        partial_kernel,
        out_shape=jax.ShapeDtypeStruct((NC, PIECE, MAPS), f32),
        in_specs=[SMEM, VMEM, VMEM],
        out_specs=VMEM,
        name="partial",
    )(place, cov, maps)


def block_spectra(place, cosines, rows, cols):
    return pl.pallas_call(
        spectra_kernel,
        out_shape=jax.ShapeDtypeStruct((L, MAPS), f32),
        in_specs=[SMEM, VMEM, VMEM, VMEM, VMEM],
        out_specs=VMEM,
        scratch_shapes=[
            pltpu.VMEM((2 * CHUNK, LANES), bf16),
            pltpu.VMEM((CHUNK, LANES), bf16),
            pltpu.VMEM((TOP, ROWS, COLS), bf16),
            pltpu.VMEM((TOP, ROWS, COLS), bf16),
            pltpu.VMEM((TOP + 1, 8, LANES), f32),
        ],
        cost_estimate=pl.CostEstimate(flops=9 * 10**9, bytes_accessed=4 * 10**6, transcendentals=0),
        name="spectra",
    )(place, cosines, rows, cols, jnp.asarray(BASIS))


def assemble(place, rows, other):
    return pl.pallas_call(
        assemble_kernel,
        out_shape=jax.ShapeDtypeStruct((MAPS, 2 * CHUNK), bf16),
        in_specs=[SMEM, VMEM, VMEM],
        out_specs=VMEM,
        scratch_shapes=[pltpu.VMEM((2 * CHUNK, MAPS), bf16)],
        name="assemble",
    )(place, rows, other).T


def everywhere(value):
    value = value + lax.ppermute(value, PROW[1], [(0, 1), (1, 0)])
    for axis in (PROW[0],) + PCOL:
        value = value + lax.ppermute(value, axis, [(0, 1), (1, 0), (2, 3), (3, 2)])
        value = value + lax.ppermute(value, axis, [(0, 3), (3, 0), (2, 1), (1, 2)])
    return value


def per_device(inverse_cov, cosines, sky_maps):
    place = jnp.stack([lax.axis_index(PROW), lax.axis_index(PCOL)]).astype(jnp.int32)
    partial = partial_products(place, inverse_cov, sky_maps.T)
    parts = lax.all_to_all(partial.astype(f16), PCOL, 0, 0, tiled=True)
    piece = jnp.sum(parts.astype(f32), axis=0).astype(bf16)

    cols = lax.ppermute(piece, ALL, TO_COLUMNS)[None]
    rows = piece[None]
    for row_step, column_step in zip(ROW_STEPS, COLUMN_STEPS):
        rows = jnp.concatenate([rows, lax.ppermute(rows, ALL, row_step)])
        cols = jnp.concatenate([cols, lax.ppermute(cols, ALL, column_step)])
    other = lax.ppermute(rows, ALL, OTHER_HALF)

    spectra = everywhere(block_spectra(place, cosines, rows, cols))
    return assemble(place, rows, other), spectra


def solution(mesh):
    split = Mesh(mesh.devices.reshape(4, 2, 4, 4), ALL)
    placed = (P(PROW, PCOL), P(PROW, PCOL), P(PCOL, None))
    return jax.shard_map(
        per_device, mesh=split, in_specs=placed, out_specs=(P(PROW, None), P()), check_vma=False
    )
```

time: 107 us -> 99.7 us (0.932)
  local copies, waits for them, and re-layouts: 7.37 us -> 0.7 us
  waiting for transfers between devices: 38.7 us -> 35.9 us
  other arithmetic: 2.71 us -> 5.21 us
  between operations: 2.01 us -> 0.76 us
    all_to_all x2 -> x0, waiting for transfers between devices: 10.1 us -> none  [from_everyone(): lax.all_to_all(copies, axis, 0, 0, axis_index_groups=groups, tiled=True)]
    ppermute x1 -> x7, starting transfers between devices: 0.63 us -> 9.91 us  [the longest x3 8.17 us: per_device(): rows = jnp.concatenate([rows, lax.ppermute(rows, ALL, row_step)])]
    all_to_all x2 -> x0, starting transfers between devices: 8.74 us -> none  [from_everyone(): lax.all_to_all(copies, axis, 0, 0, axis_index_groups=groups, tiled=True)]
    ppermute x1 -> x7, waiting for transfers between devices: 3.35 us -> 11.2 us  [the longest x3 5.95 us: per_device(): rows = jnp.concatenate([rows, lax.ppermute(rows, ALL, row_step)])]
    unnamed x6 -> x4, local copies, waits for them, and re-layouts: 3.4 us -> 0.7 us
    ppermute x3, starting transfers between devices: 2.84 us -> 0.35 us  [everywhere(): value = value + lax.ppermute(value, axis, [(0, 3), (3, 0), (2, 1), (1, 2)])]
    ppermute x3, waiting for transfers between devices: 11.7 us -> 9.75 us  [everywhere(): value = value + lax.ppermute(value, axis, [(0, 1), (1, 0), (2, 3), (3, 2)])]
    concatenate x1 -> x6, other arithmetic: 0.09 us -> 1.6 us  [the longest x3 0.8 us: per_device(): rows = jnp.concatenate([rows, lax.ppermute(rows, ALL, row_step)])]
  transfers between devices with their start and end apart: 11 -> 15, of which waited for: 10 -> 12; matrix products, arithmetic and copies ran while one was open for 3% -> 1% of each run, Pallas kernels for 0% -> 2%
where the time goes in v2:
time: 99.7 us; the launch traced here: 99.4 us
  waiting for transfers between devices  35.9 us (36%)
  Pallas kernels  23.9 us (24%)
  blocking collectives  19.3 us (19%)
  starting transfers between devices  13.5 us (14%)
  other arithmetic  5.21 us (5%)
    all_to_all x1, blocking collectives, per_device(): parts = lax.all_to_all(partial.astype(f16), PCOL, 0, 0, tiled=True)  19.3 us
    pallas_call x1, Pallas kernels, block_spectra(): pl.pallas_call(spectra_kernel, out_shape=jax.ShapeDtypeStruct((L, MAPS),...  19.2 us
    ppermute x3, waiting for transfers between devices, everywhere(): value = value + lax.ppermute(value, axis, [(0, 3), (3, 0), (2, 1), (1, 2)])  13.6 us
    ppermute x3, waiting for transfers between devices, everywhere(): value = value + lax.ppermute(value, axis, [(0, 1), (1, 0), (2, 3), (3, 2)])  9.75 us
    ppermute x3, starting transfers between devices, per_device(): rows = jnp.concatenate([rows, lax.ppermute(rows, ALL, row_step)])  8.17 us
    ppermute x3, waiting for transfers between devices, per_device(): rows = jnp.concatenate([rows, lax.ppermute(rows, ALL, row_step)])  5.95 us
    pallas_call x1, Pallas kernels, partial_products(): pl.pallas_call(partial_kernel, out_shape=jax.ShapeDtypeStruct((NC, PIECE,...  2.69 us
    ppermute x1, waiting for transfers between devices, per_device(): cols = lax.ppermute(piece, ALL, TO_COLUMNS)[None]  2.61 us
  transfers between devices with their start and end apart: 15, of which 12 were waited for; matrix products, arithmetic and copies ran while one was open for 1% of the time, Pallas kernels for 2%

profile of v2, /device:TPU:0, one launch (start us, length us, event | category | flops | bytes accessed | tf_op | source)
XLA Modules:
  0.0 99.4 jit_solution(7319918026700725400)
XLA Ops:
  0.6 0.7 pad_add_fusion.place_ref
  1.3 2.7 %partial.1 = f32[16,64,192]{2,1,0:T(8,128)} custom-call(s32[2]{0:T(128)} %pad_add_fusion.place_ref, bf16[1024,512]{1,0:T(8,128)(2,1)} %cov_ref.1, bf16[192,512]{1,0:T(8,128)(2,1)} %bitcast.15), custom_call_target="tpu_custom_call" | custom-call | tf_op jit(solution)/shard_map/partial/pallas_call | solution.py:215
  4.0 1.3 %convert_element_type.19 = f16[16,64,192]{2,1,0:T(8,128)(2,1)S(1)} convert(f32[16,64,192]{2,1,0:T(8,128)} %partial.1) | non-fusion elementwise | flops 196608 | bytes 1179648 | tf_op jit(solution)/shard_map/convert_element_type | solution.py:264
  5.3 19.3 %all_to_all.5 = f16[16,64,192]{2,1,0:T(8,128)(2,1)S(1)} all-to-all(f16[16,64,192]{2,1,0:T(8,128)(2,1)S(1)} %convert_element_type.19), channel_id=1, replica_groups=mesh['prow_0'=4,'prow_1'=2,'pcol_0'=4,'pcol_1'=4] {'pcol_0','pcol_1'}, dimensions={0} | all-to-all | bytes 786432 | tf_op jit(solution)/shard_map/all_to_all | solution.py:264
  24.6 0.1 convert_reduce_fusion
  24.7 0.6 collective-permute-start.4
  25.4 0.7 collective-permute-start
  26.1 2.6 %collective-permute-done.4 = bf16[64,192]{1,0:T(8,128)(2,1)S(1)} collective-permute-done((bf16[64,192]{1,0:T(8,128)(2,1)S(1)}, bf16[64,192]{1,0:T(8,128)(2,1)S(1)}, u32[]{:S(2)}, u32[]{:S(2)}) %collective-permute-start.4) | collective-permute-done | bytes 24608 | tf_op jit(solution)/shard_map/ppermute | solution.py:267
  28.7 0.0 collective-permute-start.5
  28.7 1.8 %collective-permute-done = bf16[1,64,192]{2,1,0:T(8,128)(2,1)S(1)} collective-permute-done((bf16[1,64,192]{2,1,0:T(8,128)(2,1)S(1)}, bf16[1,64,192]{2,1,0:T(8,128)(2,1)S(1)}, u32[]{:S(2)}, u32[]{:S(2)}) %collective-permute-start) | collective-permute-done | bytes 24608 | tf_op jit(solution)/shard_map/ppermute | solution.py:270
  30.5 2.8 %collective-permute-start.1 = (bf16[2,64,192]{2,1,0:T(8,128)(2,1)S(1)}, bf16[2,64,192]{2,1,0:T(8,128)(2,1)S(1)}, u32[]{:S(2)}, u32[]{:S(2)}) collective-permute-start(bf16[2,64,192]{2,1,0:T(8,128)(2,1)S(1)} %pad_maximum_fusion.4), channel_id=1, source_target_pairs={{1,4},{2,6},{4,1},{6,2},{8,12},{10,14},{12,8},{14,10},{0,5},{3,7},... | collective-permute-start | bytes 147464 | tf_op jit(solution)/shard_map/ppermute | solution.py:270
  33.4 0.0 collective-permute-done.5
  33.4 0.1 collective-permute-start.6
  33.5 2.3 %collective-permute-done.1 = bf16[2,64,192]{2,1,0:T(8,128)(2,1)S(1)} collective-permute-done((bf16[2,64,192]{2,1,0:T(8,128)(2,1)S(1)}, bf16[2,64,192]{2,1,0:T(8,128)(2,1)S(1)}, u32[]{:S(2)}, u32[]{:S(2)}) %collective-permute-start.1) | collective-permute-done | bytes 49184 | tf_op jit(solution)/shard_map/ppermute | solution.py:270
  35.8 4.6 %collective-permute-start.2 = (bf16[4,64,192]{2,1,0:T(8,128)(2,1)S(1)}, bf16[4,64,192]{2,1,0:T(8,128)(2,1)S(1)}, u32[]{:S(2)}, u32[]{:S(2)}) collective-permute-start(bf16[4,64,192]{2,1,0:T(8,128)(2,1)S(1)} %pad_maximum_fusion.2), channel_id=1, source_target_pairs={{1,12},{2,14},{4,8},{6,10},{8,4},{10,6},{12,1},{14,2},{0,13},{3,15... | collective-permute-start | bytes 294920 | tf_op jit(solution)/shard_map/ppermute | solution.py:270
  40.4 0.0 collective-permute-done.6
  40.4 1.0 %collective-permute-start.7 = (bf16[4,64,192]{2,1,0:T(8,128)(2,1)S(1)}, bf16[4,64,192]{2,1,0:T(8,128)(2,1)S(1)}, u32[]{:S(2)}, u32[]{:S(2)}) collective-permute-start(bf16[4,64,192]{2,1,0:T(8,128)(2,1)S(1)} %pad_maximum_fusion.3), channel_id=1, source_target_pairs={{0,96},{1,97},{2,98},{3,99},{4,100},{5,101},{6,102},{7,103},{8,104... | collective-permute-start | bytes 294920 | tf_op jit(solution)/shard_map/ppermute | solution.py:271
  41.4 1.9 %collective-permute-done.2 = bf16[4,64,192]{2,1,0:T(8,128)(2,1)S(1)} collective-permute-done((bf16[4,64,192]{2,1,0:T(8,128)(2,1)S(1)}, bf16[4,64,192]{2,1,0:T(8,128)(2,1)S(1)}, u32[]{:S(2)}, u32[]{:S(2)}) %collective-permute-start.2) | collective-permute-done | bytes 98336 | tf_op jit(solution)/shard_map/ppermute | solution.py:270
  43.3 0.8 pad_maximum_fusion.rows_ref
  44.1 2.6 %collective-permute-done.7 = bf16[4,64,192]{2,1,0:T(8,128)(2,1)S(1)} collective-permute-done((bf16[4,64,192]{2,1,0:T(8,128)(2,1)S(1)}, bf16[4,64,192]{2,1,0:T(8,128)(2,1)S(1)}, u32[]{:S(2)}, u32[]{:S(2)}) %collective-permute-start.7) | collective-permute-done | bytes 98336 | tf_op jit(solution)/shard_map/ppermute | solution.py:271
  46.7 0.8 pad_maximum_fusion.1.cols_ref
  47.4 0.0 copy-start
  47.4 19.2 %spectra.1 = f32[64,192]{1,0:T(8,128)} custom-call(s32[2]{0:T(128)} %pad_add_fusion.place_ref, f32[1024,512]{1,0:T(8,128)} %cos_ref.1, bf16[8,64,192]{2,1,0:T(8,128)(2,1)} %pad_maximum_fusion.rows_ref, bf16[8,64,192]{2,1,0:T(8,128)(2,1)} %pad_maximum_fusion.1.cols_ref, f32[64,528]{1,0:T(8,128)} %constant.25.clone.basis_ref), custom_call_target="tpu_custom_call" | custom-call | flops 8999999488 | bytes 4000000 | tf_op jit(solution)/shard_map/spectra/pallas_call | solution.py:225
  66.6 0.0 collective-permute-start.8
  66.6 1.5 %collective-permute-done.8 = f32[64,192]{1,0:T(8,128)S(1)} collective-permute-done((f32[64,192]{1,0:T(8,128)}, f32[64,192]{1,0:T(8,128)S(1)}, u32[]{:S(2)}, u32[]{:S(2)}) %collective-permute-start.8) | collective-permute-done | bytes 49184 | tf_op jit(solution)/shard_map/ppermute | solution.py:254
  68.1 0.9 add.29
  69.0 0.1 collective-permute-start.9
  69.1 4.3 %collective-permute-done.9 = f32[64,192]{1,0:T(8,128)S(1)} collective-permute-done((f32[64,192]{1,0:T(8,128)S(1)}, f32[64,192]{1,0:T(8,128)S(1)}, u32[]{:S(2)}, u32[]{:S(2)}) %collective-permute-start.9) | collective-permute-done | bytes 49184 | tf_op jit(solution)/shard_map/ppermute | solution.py:256
  73.3 0.1 collective-permute-start.10
  73.4 5.5 %collective-permute-done.10 = f32[64,192]{1,0:T(8,128)S(1)} collective-permute-done((f32[64,192]{1,0:T(8,128)S(1)}, f32[64,192]{1,0:T(8,128)S(1)}, u32[]{:S(2)}, u32[]{:S(2)}) %collective-permute-start.10) | collective-permute-done | bytes 49184 | tf_op jit(solution)/shard_map/ppermute | solution.py:257
  78.9 0.1 collective-permute-start.11
  79.0 0.0 copy-done
  79.0 1.5 %collective-permute-start.3 = (bf16[8,64,192]{2,1,0:T(8,128)(2,1)S(1)}, bf16[8,64,192]{2,1,0:T(8,128)(2,1)S(1)}, u32[]{:S(2)}, u32[]{:S(2)}) collective-permute-start(bf16[8,64,192]{2,1,0:T(8,128)(2,1)S(1)} %copy-done), channel_id=1, source_target_pairs={{1,0},{2,3},{4,5},{6,7},{8,9},{10,11},{12,13},{14,15},{0,1},{3,2},... | collective-permute-start | bytes 589832 | tf_op jit(solution)/shard_map/ppermute | solution.py:272
  80.5 2.7 %collective-permute-done.11 = f32[64,192]{1,0:T(8,128)S(1)} collective-permute-done((f32[64,192]{1,0:T(8,128)S(1)}, f32[64,192]{1,0:T(8,128)S(1)}, u32[]{:S(2)}, u32[]{:S(2)}) %collective-permute-start.11) | collective-permute-done | bytes 49184 | tf_op jit(solution)/shard_map/ppermute | solution.py:256
  83.2 0.2 collective-permute-start.12
  83.4 5.4 %collective-permute-done.12 = f32[64,192]{1,0:T(8,128)S(1)} collective-permute-done((f32[64,192]{1,0:T(8,128)S(1)}, f32[64,192]{1,0:T(8,128)S(1)}, u32[]{:S(2)}, u32[]{:S(2)}) %collective-permute-start.12) | collective-permute-done | bytes 49184 | tf_op jit(solution)/shard_map/ppermute | solution.py:257
  88.8 1.5 %collective-permute-start.13 = (f32[64,192]{1,0:T(8,128)S(1)}, f32[64,192]{1,0:T(8,128)S(1)}, u32[]{:S(2)}, u32[]{:S(2)}) collective-permute-start(f32[64,192]{1,0:T(8,128)S(1)} %add.33), channel_id=1, source_target_pairs={{0,1},{1,0},{2,3},{3,2},{4,5},{5,4},{6,7},{7,6},{8,9},{9,8},{10,11... | collective-permute-start | bytes 147464 | tf_op jit(solution)/shard_map/ppermute | solution.py:256
  90.4 2.8 %collective-permute-done.13 = f32[64,192]{1,0:T(8,128)S(1)} collective-permute-done((f32[64,192]{1,0:T(8,128)S(1)}, f32[64,192]{1,0:T(8,128)S(1)}, u32[]{:S(2)}, u32[]{:S(2)}) %collective-permute-start.13) | collective-permute-done | bytes 49184 | tf_op jit(solution)/shard_map/ppermute | solution.py:256
  93.2 0.1 collective-permute-start.14
  93.3 0.0 collective-permute-done.3.other_ref
  93.3 0.0 copy-start.1
  93.3 0.7 copy-done.1
  94.0 2.0 %assemble.1 = bf16[192,1024]{1,0:T(8,128)(2,1)} custom-call(s32[2]{0:T(128)} %pad_add_fusion.place_ref, bf16[8,64,192]{2,1,0:T(8,128)(2,1)} %pad_maximum_fusion.rows_ref, bf16[8,64,192]{2,1,0:T(8,128)(2,1)} %copy-done.1), custom_call_target="tpu_custom_call" | custom-call | tf_op jit(solution)/shard_map/assemble/pallas_call | solution.py:243
  96.0 2.7 %collective-permute-done.14 = f32[64,192]{1,0:T(8,128)S(1)} collective-permute-done((f32[64,192]{1,0:T(8,128)S(1)}, f32[64,192]{1,0:T(8,128)S(1)}, u32[]{:S(2)}, u32[]{:S(2)}) %collective-permute-start.14) | collective-permute-done | bytes 49184 | tf_op jit(solution)/shard_map/ppermute | solution.py:257
  98.7 0.6 add.35
  (9 shorter events, 0.1 us)
Async XLA Ops:
  24.7 4.0 %collective-permute-start.4 = (bf16[64,192]{1,0:T(8,128)(2,1)S(1)}, bf16[64,192]{1,0:T(8,128)(2,1)S(1)}, u32[]{:S(2)}, u32[]{:S(2)}) collective-permute-start(bf16[64,192]{1,0:T(8,128)(2,1)S(1)} %convert_reduce_fusion), channel_id=1, source_target_pairs={{1,0},{2,16},{4,32},{6,48},{8,64},{10,80},{12,96},{14,112},{0,1},{... | collective-permute-start | bytes 73736 | tf_op jit(solution)/shard_map/ppermute | solution.py:267
  25.4 5.1 %collective-permute-start = (bf16[1,64,192]{2,1,0:T(8,128)(2,1)S(1)}, bf16[1,64,192]{2,1,0:T(8,128)(2,1)S(1)}, u32[]{:S(2)}, u32[]{:S(2)}) collective-permute-start(bf16[1,64,192]{2,1,0:T(8,128)(2,1)S(1)} %bitcast.6), channel_id=1, source_target_pairs={{1,2},{2,1},{4,6},{6,4},{8,10},{10,8},{12,14},{14,12},{0,3},{3,0},... | collective-permute-start | bytes 73736 | tf_op jit(solution)/shard_map/ppermute | solution.py:270
  28.7 4.6 %collective-permute-start.5 = (bf16[1,64,192]{2,1,0:T(8,128)(2,1)S(1)}, bf16[1,64,192]{2,1,0:T(8,128)(2,1)S(1)}, u32[]{:S(2)}, u32[]{:S(2)}) collective-permute-start(bf16[1,64,192]{2,1,0:T(8,128)(2,1)S(1)} %bitcast.11), channel_id=1, source_target_pairs={{0,16},{1,17},{2,18},{3,19},{4,20},{5,21},{6,22},{7,23},{8,24},{9,... | collective-permute-start | bytes 73736 | tf_op jit(solution)/shard_map/ppermute | solution.py:271
  30.5 5.2 %collective-permute-start.1 = (bf16[2,64,192]{2,1,0:T(8,128)(2,1)S(1)}, bf16[2,64,192]{2,1,0:T(8,128)(2,1)S(1)}, u32[]{:S(2)}, u32[]{:S(2)}) collective-permute-start(bf16[2,64,192]{2,1,0:T(8,128)(2,1)S(1)} %pad_maximum_fusion.4), channel_id=1, source_target_pairs={{1,4},{2,6},{4,1},{6,2},{8,12},{10,14},{12,8},{14,10},{0,5},{3,7},... | collective-permute-start | bytes 147464 | tf_op jit(solution)/shard_map/ppermute | solution.py:270
  33.4 7.0 %collective-permute-start.6 = (bf16[2,64,192]{2,1,0:T(8,128)(2,1)S(1)}, bf16[2,64,192]{2,1,0:T(8,128)(2,1)S(1)}, u32[]{:S(2)}, u32[]{:S(2)}) collective-permute-start(bf16[2,64,192]{2,1,0:T(8,128)(2,1)S(1)} %pad_maximum_fusion.5), channel_id=1, source_target_pairs={{0,32},{1,33},{2,34},{3,35},{4,36},{5,37},{6,38},{7,39},{8,40},{9,... | collective-permute-start | bytes 147464 | tf_op jit(solution)/shard_map/ppermute | solution.py:271
  35.8 7.5 %collective-permute-start.2 = (bf16[4,64,192]{2,1,0:T(8,128)(2,1)S(1)}, bf16[4,64,192]{2,1,0:T(8,128)(2,1)S(1)}, u32[]{:S(2)}, u32[]{:S(2)}) collective-permute-start(bf16[4,64,192]{2,1,0:T(8,128)(2,1)S(1)} %pad_maximum_fusion.2), channel_id=1, source_target_pairs={{1,12},{2,14},{4,8},{6,10},{8,4},{10,6},{12,1},{14,2},{0,13},{3,15... | collective-permute-start | bytes 294920 | tf_op jit(solution)/shard_map/ppermute | solution.py:270
  40.4 6.3 %collective-permute-start.7 = (bf16[4,64,192]{2,1,0:T(8,128)(2,1)S(1)}, bf16[4,64,192]{2,1,0:T(8,128)(2,1)S(1)}, u32[]{:S(2)}, u32[]{:S(2)}) collective-permute-start(bf16[4,64,192]{2,1,0:T(8,128)(2,1)S(1)} %pad_maximum_fusion.3), channel_id=1, source_target_pairs={{0,96},{1,97},{2,98},{3,99},{4,100},{5,101},{6,102},{7,103},{8,104... | collective-permute-start | bytes 294920 | tf_op jit(solution)/shard_map/ppermute | solution.py:271
  47.4 31.5 %copy-start = (bf16[8,64,192]{2,1,0:T(8,128)(2,1)S(1)}, bf16[8,64,192]{2,1,0:T(8,128)(2,1)}, u32[]{:S(2)}) copy-start(bf16[8,64,192]{2,1,0:T(8,128)(2,1)} %pad_maximum_fusion.rows_ref) | copy-start | bytes 589828
  66.6 1.5 %collective-permute-start.8 = (f32[64,192]{1,0:T(8,128)}, f32[64,192]{1,0:T(8,128)S(1)}, u32[]{:S(2)}, u32[]{:S(2)}) collective-permute-start(f32[64,192]{1,0:T(8,128)} %spectra.1), channel_id=1, source_target_pairs={{0,16},{16,0},{1,17},{17,1},{2,18},{18,2},{3,19},{19,3},{4,20},{20... | collective-permute-start | bytes 147464 | tf_op jit(solution)/shard_map/ppermute | solution.py:254
  69.0 4.3 %collective-permute-start.9 = (f32[64,192]{1,0:T(8,128)S(1)}, f32[64,192]{1,0:T(8,128)S(1)}, u32[]{:S(2)}, u32[]{:S(2)}) collective-permute-start(f32[64,192]{1,0:T(8,128)S(1)} %add.29), channel_id=1, source_target_pairs={{0,32},{32,0},{64,96},{96,64},{1,33},{33,1},{65,97},{97,65},{2,34}... | collective-permute-start | bytes 147464 | tf_op jit(solution)/shard_map/ppermute | solution.py:256
  73.3 5.6 %collective-permute-start.10 = (f32[64,192]{1,0:T(8,128)S(1)}, f32[64,192]{1,0:T(8,128)S(1)}, u32[]{:S(2)}, u32[]{:S(2)}) collective-permute-start(f32[64,192]{1,0:T(8,128)S(1)} %add.30), channel_id=1, source_target_pairs={{0,96},{96,0},{64,32},{32,64},{1,97},{97,1},{65,33},{33,65},{2,98}... | collective-permute-start | bytes 147464 | tf_op jit(solution)/shard_map/ppermute | solution.py:257
  78.9 4.3 %collective-permute-start.11 = (f32[64,192]{1,0:T(8,128)S(1)}, f32[64,192]{1,0:T(8,128)S(1)}, u32[]{:S(2)}, u32[]{:S(2)}) collective-permute-start(f32[64,192]{1,0:T(8,128)S(1)} %add.31), channel_id=1, source_target_pairs={{0,4},{4,0},{8,12},{12,8},{1,5},{5,1},{9,13},{13,9},{2,6},{6,2},{1... | collective-permute-start | bytes 147464 | tf_op jit(solution)/shard_map/ppermute | solution.py:256
  79.0 14.3 %collective-permute-start.3 = (bf16[8,64,192]{2,1,0:T(8,128)(2,1)S(1)}, bf16[8,64,192]{2,1,0:T(8,128)(2,1)S(1)}, u32[]{:S(2)}, u32[]{:S(2)}) collective-permute-start(bf16[8,64,192]{2,1,0:T(8,128)(2,1)S(1)} %copy-done), channel_id=1, source_target_pairs={{1,0},{2,3},{4,5},{6,7},{8,9},{10,11},{12,13},{14,15},{0,1},{3,2},... | collective-permute-start | bytes 589832 | tf_op jit(solution)/shard_map/ppermute | solution.py:272
  83.2 5.6 %collective-permute-start.12 = (f32[64,192]{1,0:T(8,128)S(1)}, f32[64,192]{1,0:T(8,128)S(1)}, u32[]{:S(2)}, u32[]{:S(2)}) collective-permute-start(f32[64,192]{1,0:T(8,128)S(1)} %add.32), channel_id=1, source_target_pairs={{0,12},{12,0},{8,4},{4,8},{1,13},{13,1},{9,5},{5,9},{2,14},{14,2},... | collective-permute-start | bytes 147464 | tf_op jit(solution)/shard_map/ppermute | solution.py:257
  88.8 4.3 %collective-permute-start.13 = (f32[64,192]{1,0:T(8,128)S(1)}, f32[64,192]{1,0:T(8,128)S(1)}, u32[]{:S(2)}, u32[]{:S(2)}) collective-permute-start(f32[64,192]{1,0:T(8,128)S(1)} %add.33), channel_id=1, source_target_pairs={{0,1},{1,0},{2,3},{3,2},{4,5},{5,4},{6,7},{7,6},{8,9},{9,8},{10,11... | collective-permute-start | bytes 147464 | tf_op jit(solution)/shard_map/ppermute | solution.py:256
  93.2 5.6 %collective-permute-start.14 = (f32[64,192]{1,0:T(8,128)S(1)}, f32[64,192]{1,0:T(8,128)S(1)}, u32[]{:S(2)}, u32[]{:S(2)}) collective-permute-start(f32[64,192]{1,0:T(8,128)S(1)} %add.34), channel_id=1, source_target_pairs={{0,3},{3,0},{2,1},{1,2},{4,7},{7,4},{6,5},{5,6},{8,11},{11,8},{10,... | collective-permute-start | bytes 147464 | tf_op jit(solution)/shard_map/ppermute | solution.py:257
  93.3 0.7 copy-start.1

commit v3 on v2

--- a/solution.py
+++ b/solution.py
@@ -22,6 +22,9 @@
 COLS = 256
 LOW = 9
 CENTRES = (18, 37, 56)
+CENTRE = 2 * LOW - 1
+FACTORS = CENTRE + 2 * len(CENTRES)
+LAG = 28
 PROW = ("prow_0", "prow_1")
 PCOL = ("pcol_0", "pcol_1")
 ALL = PROW + PCOL
@@ -66,40 +69,54 @@
         columns += [cheb[:, n - a] - cheb[:, n + a] for a in range(1, LOW + 1)]
     matrix = np.stack(columns, axis=1)
     assert matrix.shape == (L, TOP + 1)
-    return np.repeat(matrix, 8, axis=1).astype(np.float32)
+    return matrix.astype(np.float32)
 
 
 BASIS = basis_matrix()
 
 
-def basis_functions(x):
+def factors(x):
     y = x + x
     t, u = [jnp.ones_like(x), x], [jnp.ones_like(x), y]
+    yield 0, x.astype(bf16)
+    yield LOW, y.astype(bf16)
     for k in range(2, LOW + 1):
         t.append(y * t[k - 1] - t[k - 2])
+        yield k - 1, t[k].astype(bf16)
         if k < LOW:
             u.append(y * u[k - 1] - u[k - 2])
+            yield LOW + k - 1, u[k].astype(bf16)
+    t9, u8 = t[9], u[8]
     square = 1.0 - x * x
-    double = t[9] + t[9]
-    t18, u17 = double * t[9] - 1.0, double * u[8]
+    double = t9 + t9
+    t18, u17 = double * t9 - 1.0, double * u8
     v18 = square * u17
+    yield CENTRE, t18.astype(bf16)
+    yield CENTRE + 1, v18.astype(bf16)
     double = t18 + t18
     t36, v36 = double * t18 - 1.0, double * v18
     t37, v37 = t36 * x - v36, v36 * x + t36 * square
+    yield CENTRE + 2, t37.astype(bf16)
+    yield CENTRE + 3, v37.astype(bf16)
     t19, u18 = t18 * x - v18, u17 * x + t18
     v19 = square * u18
     t56, v56 = t37 * t19 - v37 * u18, v37 * t19 + t37 * v19
-    low_t = [None] + [value.astype(bf16) for value in t[1:]]
-    low_u = [None] + [value.astype(bf16) for value in u[1:]]
-    yield from low_t[1:LOW]
-    for tn, vn in ((t18, v18), (t37, v37), (t56, v56)):
-        tn, vn = tn.astype(bf16), vn.astype(bf16)
-        yield tn
-        for a in range(1, LOW + 1):
-            yield tn * low_t[a]
-        yield vn
-        for a in range(2, LOW + 1):
-            yield vn * low_u[a - 1]
+    yield CENTRE + 4, t56.astype(bf16)
+    yield CENTRE + 5, v56.astype(bf16)
+
+
+def basis_function(k, made):
+    if k < LOW - 1:
+        return made[k]
+    centre, which = divmod(k - (LOW - 1), 2 * LOW + 1)
+    tn, vn = CENTRE + 2 * centre, CENTRE + 2 * centre + 1
+    if which == 0:
+        return made[tn]
+    if which <= LOW:
+        return made[tn] * made[which - 1]
+    if which == LOW + 1:
+        return made[vn]
+    return made[vn] * made[LOW + which - LOW - 2]
 
 
 def partial_kernel(place_ref, cov_ref, maps_ref, out_ref):
@@ -116,7 +133,29 @@
 
 
 def spectra_kernel(
-    place_ref, cos_ref, rows_ref, cols_ref, basis_ref, out_ref, maps, weights, even, odd, total
+    place_ref, cos_ref, r0, r1, r2, r3, c0, c1, c2, c3, basis_ref, out_ref,
+    maps, weights, even, odd, total,
+):
+    def with_sums(*sums):
+        spectra_body(
+            place_ref, cos_ref, (r0, r1, r2, r3), (c0, c1, c2, c3), basis_ref, out_ref,
+            maps, weights, even, odd, total, (sums[:17], sums[17:]),
+        )
+
+    pl.run_scoped(
+        with_sums,
+        *[pltpu.ACC(0)((ROWS, LANES), f32)] * 17,
+        *[pltpu.ACC(1)((ROWS, LANES), f32)] * 16,
+    )
+
+
+def pieces_of(refs):
+    return [(ref, at) for ref in refs for at in range(ref.shape[0])]
+
+
+def spectra_body(
+    place_ref, cos_ref, rows_refs, cols_refs, basis_ref, out_ref,
+    maps, weights, even, odd, total, sums,
 ):
     r, c = place_ref[0], place_ref[1]
     group, own = c // 2, c % 2
@@ -125,14 +164,13 @@
     half = jnp.where(group > r, own, other)
     zeros = jnp.zeros((PIECE, LANES - MAPS), bf16)
     row_sum = col_sum = jnp.zeros((8, LANES), f32)
-    for place in range(NR):
-        rows = jnp.concatenate([rows_ref[place], zeros], axis=1)
-        at = pl.multiple_of((group ^ ORDER[place]) * PIECE, PIECE)
-        maps[pl.ds(at, PIECE)] = rows
-        cols = jnp.concatenate([cols_ref[place], zeros], axis=1)
-        at = pl.multiple_of((r ^ ORDER[place]) * PIECE, PIECE)
-        weights[pl.ds(at, PIECE)] = cols
-        maps[pl.ds(CHUNK + at, PIECE)] = cols
+    for order, (rows_ref, at), (cols_ref, _) in zip(ORDER, pieces_of(rows_refs), pieces_of(cols_refs)):
+        rows = jnp.concatenate([rows_ref[at], zeros], axis=1)
+        maps[pl.ds(pl.multiple_of((group ^ order) * PIECE, PIECE), PIECE)] = rows
+        cols = jnp.concatenate([cols_ref[at], zeros], axis=1)
+        to = pl.multiple_of((r ^ order) * PIECE, PIECE)
+        weights[pl.ds(to, PIECE)] = cols
+        maps[pl.ds(CHUNK + to, PIECE)] = cols
         row_sum += jnp.sum(rows.astype(f32).reshape(PIECE // 8, 8, LANES), axis=0)
         col_sum += jnp.sum(cols.astype(f32).reshape(PIECE // 8, 8, LANES), axis=0)
     row_sum = jnp.sum(row_sum, axis=0, keepdims=True)
@@ -141,6 +179,7 @@
     beta = jnp.where(diagonal, 0.5, 0.0)
     total[...] = jnp.zeros_like(total)
     total[0, 0:1] = col_sum * (alpha * row_sum + beta * col_sum)
+    count = jnp.where(diagonal, 40, 32)
 
     def tile(t):
         part, first = t // 8, 32 * (t % 8)
@@ -165,44 +204,77 @@
         column = pl.multiple_of(column * COLS, COLS)
         for first in range(0, ROWS, 16):
             x = cos_ref[pl.ds(cos_row + first, 16), pl.ds(column, COLS)]
-            for k, value in enumerate(basis_functions(x)):
-                slot[k, first : first + 16] = value
-
-    def contract(t, slot):
-        _, map_row, column, weight = tile(t)
-        left = maps[pl.ds(pl.multiple_of(map_row, ROWS), ROWS)].astype(f32) * weight
+            for which, value in factors(x):
+                slot[which, first : first + 16] = value
+                yield
+
+    def stage(t):
+        column = tile(t)[2]
         right = weights[pl.ds(pl.multiple_of(column * COLS, COLS), COLS)]
-        image = jnp.dot(slot[...].reshape(TOP * ROWS, COLS), right, preferred_element_type=f32)
+        for unit in range(2):
+            pltpu.matmul_push_rhs(right, 0, unit)
+
+    def left_of(t):
+        _, map_row, _, weight = tile(t)
+        return maps[pl.ds(pl.multiple_of(map_row, ROWS), ROWS)].astype(f32) * weight
+
+    def sum_of(k):
+        unit, turn = k % 2, k // 2
+        return sums[unit][turn % 16 if turn < 32 else 16]
+
+    def take(k, left):
+        product = pltpu.matmul_pop(sum_of(k)) * left
+        total[k + 1] += jnp.sum(product.reshape(ROWS // 8, 8, LANES), axis=0)
+
+    def process(t, now, later):
+        following = jnp.minimum(t + 1, count - 1)
+        making = generate(following, later)
+        left = left_of(jnp.maximum(t - 1, 0))
         for k in range(TOP):
-            product = image[ROWS * k : ROWS * (k + 1)] * left
-            total[k + 1] += jnp.sum(product.reshape(ROWS // 8, 8, LANES), axis=0)
-
-    count = jnp.where(diagonal, 40, 32)
-    generate(0, even)
+            take((k - LAG) % TOP, left)
+            if k == LAG - 1:
+                left = left_of(t)
+            pltpu.matmul_acc_lhs(
+                sum_of(k), basis_function(k, now), load_staged_rhs=0 if k < 2 else None
+            )
+            if k == 8:
+                stage(following)
+            next(making, None)
+        for _ in making:
+            pass
+
+    for one in sums[0] + sums[1]:
+        pltpu.matmul_pop(one)
+    for _ in generate(0, even):
+        pass
+    stage(0)
 
     def step(pair, carry):
-        t = 2 * pair
-        generate(t + 1, odd)
-        contract(t, even)
-        generate(jnp.minimum(t + 2, count - 1), even)
-        contract(t + 1, odd)
+        process(2 * pair, even, odd)
+        process(2 * pair + 1, odd, even)
         return carry
 
     lax.fori_loop(0, count // 2, step, 0)
-    sums = total[...].reshape((TOP + 1) * 8, LANES)
-    spectra = jnp.dot(
-        basis_ref[...], sums, preferred_element_type=f32, precision=lax.Precision.HIGHEST
-    )
+    left = left_of(count - 1)
+    for k in range(TOP - LAG, TOP):
+        take(k, left)
+    for unit in range(2):
+        pltpu.matmul_acc_lhs(sums[unit][0], jnp.zeros((ROWS, COLS), bf16), load_staged_rhs=0)
+        pltpu.matmul_pop(sums[unit][0])
+
+    spectra = jnp.zeros((L, LANES), f32)
+    for k in range(TOP + 1):
+        spectra += basis_ref[:, k : k + 1] * jnp.sum(total[k], axis=0, keepdims=True)
     out_ref[...] = spectra[:, :MAPS]
 
 
-def assemble_kernel(place_ref, rows_ref, other_ref, out_ref, scratch):
+def assemble_kernel(place_ref, r0, r1, r2, r3, other_ref, out_ref, scratch):
     r, c = place_ref[0], place_ref[1]
     group = c // 2
     half = jnp.where(group > r, c % 2, 1 - c % 2)
-    for place in range(NR):
+    for place, (ref, one) in enumerate(pieces_of((r0, r1, r2, r3))):
         at = (group ^ ORDER[place]) * PIECE
-        scratch[pl.ds(pl.multiple_of(CHUNK * half + at, PIECE), PIECE)] = rows_ref[place]
+        scratch[pl.ds(pl.multiple_of(CHUNK * half + at, PIECE), PIECE)] = ref[one]
         scratch[pl.ds(pl.multiple_of(CHUNK * (1 - half) + at, PIECE), PIECE)] = other_ref[place]
     out_ref[...] = scratch[...].T
 
@@ -225,29 +297,29 @@
     return pl.pallas_call(
         spectra_kernel,
         out_shape=jax.ShapeDtypeStruct((L, MAPS), f32),
-        in_specs=[SMEM, VMEM, VMEM, VMEM, VMEM],
+        in_specs=[SMEM] + [VMEM] * 10,
         out_specs=VMEM,
         scratch_shapes=[
             pltpu.VMEM((2 * CHUNK, LANES), bf16),
             pltpu.VMEM((CHUNK, LANES), bf16),
-            pltpu.VMEM((TOP, ROWS, COLS), bf16),
-            pltpu.VMEM((TOP, ROWS, COLS), bf16),
+            pltpu.VMEM((FACTORS, ROWS, COLS), bf16),
+            pltpu.VMEM((FACTORS, ROWS, COLS), bf16),
             pltpu.VMEM((TOP + 1, 8, LANES), f32),
         ],
         cost_estimate=pl.CostEstimate(flops=9 * 10**9, bytes_accessed=4 * 10**6, transcendentals=0),
         name="spectra",
-    )(place, cosines, rows, cols, jnp.asarray(BASIS))
+    )(place, cosines, *rows, *cols, jnp.asarray(BASIS))
 
 
 def assemble(place, rows, other):
     return pl.pallas_call(
         assemble_kernel,
         out_shape=jax.ShapeDtypeStruct((MAPS, 2 * CHUNK), bf16),
-        in_specs=[SMEM, VMEM, VMEM],
+        in_specs=[SMEM] + [VMEM] * 5,
         out_specs=VMEM,
         scratch_shapes=[pltpu.VMEM((2 * CHUNK, MAPS), bf16)],
         name="assemble",
-    )(place, rows, other).T
+    )(place, *rows, other).T
 
 
 def everywhere(value):
@@ -264,12 +336,11 @@
     parts = lax.all_to_all(partial.astype(f16), PCOL, 0, 0, tiled=True)
     piece = jnp.sum(parts.astype(f32), axis=0).astype(bf16)
 
-    cols = lax.ppermute(piece, ALL, TO_COLUMNS)[None]
-    rows = piece[None]
+    cols, rows = [lax.ppermute(piece, ALL, TO_COLUMNS)[None]], [piece[None]]
     for row_step, column_step in zip(ROW_STEPS, COLUMN_STEPS):
-        rows = jnp.concatenate([rows, lax.ppermute(rows, ALL, row_step)])
-        cols = jnp.concatenate([cols, lax.ppermute(cols, ALL, column_step)])
-    other = lax.ppermute(rows, ALL, OTHER_HALF)
+        rows.append(lax.ppermute(jnp.concatenate(rows), ALL, row_step))
+        cols.append(lax.ppermute(jnp.concatenate(cols), ALL, column_step))
+    other = lax.ppermute(jnp.concatenate(rows), ALL, OTHER_HALF)
 
     spectra = everywhere(block_spectra(place, cosines, rows, cols))
     return assemble(place, rows, other), spectra

time: 99.7 us -> 99.2 us (level)
  no operation moved by 1% of the time
where the time goes in v3:
time: 99.2 us; the launch traced here: 98.9 us
  waiting for transfers between devices  35.7 us (36%)
  Pallas kernels  23.7 us (24%)
  blocking collectives  19.3 us (19%)
  starting transfers between devices  13.5 us (14%)
  other arithmetic  4.55 us (5%)
  local copies, waits for them, and re-layouts  1.36 us (1%)
    all_to_all x1, blocking collectives, per_device(): parts = lax.all_to_all(partial.astype(f16), PCOL, 0, 0, tiled=True)  19.3 us
    pallas_call x1, Pallas kernels, block_spectra(): pl.pallas_call(spectra_kernel, out_shape=jax.ShapeDtypeStruct((L, MAPS),...  18.9 us
    ppermute x3, waiting for transfers between devices, everywhere(): value = value + lax.ppermute(value, axis, [(0, 3), (3, 0), (2, 1), (1, 2)])  13.5 us
    ppermute x3, waiting for transfers between devices, everywhere(): value = value + lax.ppermute(value, axis, [(0, 1), (1, 0), (2, 3), (3, 2)])  8.77 us
    ppermute x3, starting transfers between devices, per_device(): rows.append(lax.ppermute(jnp.concatenate(rows), ALL, row_step))  8.17 us
    ppermute x3, waiting for transfers between devices, per_device(): rows.append(lax.ppermute(jnp.concatenate(rows), ALL, row_step))  5.95 us
    ppermute x3, waiting for transfers between devices, per_device(): cols.append(lax.ppermute(jnp.concatenate(cols), ALL, column_step))  3.35 us
    pallas_call x1, Pallas kernels, partial_products(): pl.pallas_call(partial_kernel, out_shape=jax.ShapeDtypeStruct((NC, PIECE,...  2.69 us
  transfers between devices with their start and end apart: 15, of which 12 were waited for; matrix products, arithmetic and copies ran while one was open for 1% of the time, Pallas kernels for 2%

profile of v3, /device:TPU:0, one launch (start us, length us, event | category | flops | bytes accessed | tf_op | source)
XLA Modules:
  0.0 98.9 jit_solution(17086828320756035541)
XLA Ops:
  0.6 0.6 pad_add_fusion.place_ref
  1.2 2.7 %partial.1 = f32[16,64,192]{2,1,0:T(8,128)} custom-call(s32[2]{0:T(128)} %pad_add_fusion.place_ref, bf16[1024,512]{1,0:T(8,128)(2,1)} %cov_ref.1, bf16[192,512]{1,0:T(8,128)(2,1)} %bitcast.13), custom_call_target="tpu_custom_call" | custom-call | tf_op jit(solution)/shard_map/partial/pallas_call | solution.py:287
  3.9 1.3 %convert_element_type.19 = f16[16,64,192]{2,1,0:T(8,128)(2,1)S(1)} convert(f32[16,64,192]{2,1,0:T(8,128)} %partial.1) | non-fusion elementwise | flops 196608 | bytes 1179648 | tf_op jit(solution)/shard_map/convert_element_type | solution.py:336
  5.2 19.3 %all_to_all.5 = f16[16,64,192]{2,1,0:T(8,128)(2,1)S(1)} all-to-all(f16[16,64,192]{2,1,0:T(8,128)(2,1)S(1)} %convert_element_type.19), channel_id=1, replica_groups=mesh['prow_0'=4,'prow_1'=2,'pcol_0'=4,'pcol_1'=4] {'pcol_0','pcol_1'}, dimensions={0} | all-to-all | bytes 786432 | tf_op jit(solution)/shard_map/all_to_all | solution.py:336
  24.5 0.1 convert_reduce_fusion
  24.6 0.6 collective-permute-start.4
  25.3 0.7 collective-permute-start
  26.0 2.6 %collective-permute-done.4 = bf16[64,192]{1,0:T(8,128)(2,1)S(1)} collective-permute-done((bf16[64,192]{1,0:T(8,128)(2,1)S(1)}, bf16[64,192]{1,0:T(8,128)(2,1)S(1)}, u32[]{:S(2)}, u32[]{:S(2)}) %collective-permute-start.4) | collective-permute-done | bytes 24608 | tf_op jit(solution)/shard_map/ppermute | solution.py:339
  28.6 0.0 collective-permute-start.5
  28.6 1.8 %collective-permute-done.r1 = bf16[1,64,192]{2,1,0:T(8,128)(2,1)S(1)} collective-permute-done((bf16[1,64,192]{2,1,0:T(8,128)(2,1)S(1)}, bf16[1,64,192]{2,1,0:T(8,128)(2,1)S(1)}, u32[]{:S(2)}, u32[]{:S(2)}) %collective-permute-start) | collective-permute-done | bytes 24608 | tf_op jit(solution)/shard_map/ppermute | solution.py:341
  30.4 2.8 %collective-permute-start.1 = (bf16[2,64,192]{2,1,0:T(8,128)(2,1)S(1)}, bf16[2,64,192]{2,1,0:T(8,128)(2,1)S(1)}, u32[]{:S(2)}, u32[]{:S(2)}) collective-permute-start(bf16[2,64,192]{2,1,0:T(8,128)(2,1)S(1)} %pad_maximum_fusion.3), channel_id=1, source_target_pairs={{1,4},{2,6},{4,1},{6,2},{8,12},{10,14},{12,8},{14,10},{0,5},{3,7},... | collective-permute-start | bytes 147464 | tf_op jit(solution)/shard_map/ppermute | solution.py:341
  33.3 0.0 collective-permute-done.5.c1
  33.3 0.1 collective-permute-start.6
  33.4 2.3 %collective-permute-done.1.r2 = bf16[2,64,192]{2,1,0:T(8,128)(2,1)S(1)} collective-permute-done((bf16[2,64,192]{2,1,0:T(8,128)(2,1)S(1)}, bf16[2,64,192]{2,1,0:T(8,128)(2,1)S(1)}, u32[]{:S(2)}, u32[]{:S(2)}) %collective-permute-start.1) | collective-permute-done | bytes 49184 | tf_op jit(solution)/shard_map/ppermute | solution.py:341
  35.7 4.6 %collective-permute-start.2 = (bf16[4,64,192]{2,1,0:T(8,128)(2,1)S(1)}, bf16[4,64,192]{2,1,0:T(8,128)(2,1)S(1)}, u32[]{:S(2)}, u32[]{:S(2)}) collective-permute-start(bf16[4,64,192]{2,1,0:T(8,128)(2,1)S(1)} %pad_maximum_fusion.1), channel_id=1, source_target_pairs={{1,12},{2,14},{4,8},{6,10},{8,4},{10,6},{12,1},{14,2},{0,13},{3,15... | collective-permute-start | bytes 294920 | tf_op jit(solution)/shard_map/ppermute | solution.py:341
  40.3 0.0 collective-permute-done.6.c2
  40.3 1.0 %collective-permute-start.7 = (bf16[4,64,192]{2,1,0:T(8,128)(2,1)S(1)}, bf16[4,64,192]{2,1,0:T(8,128)(2,1)S(1)}, u32[]{:S(2)}, u32[]{:S(2)}) collective-permute-start(bf16[4,64,192]{2,1,0:T(8,128)(2,1)S(1)} %pad_maximum_fusion.2), channel_id=1, source_target_pairs={{0,96},{1,97},{2,98},{3,99},{4,100},{5,101},{6,102},{7,103},{8,104... | collective-permute-start | bytes 294920 | tf_op jit(solution)/shard_map/ppermute | solution.py:342
  41.3 1.9 %collective-permute-done.2.r3 = bf16[4,64,192]{2,1,0:T(8,128)(2,1)S(1)} collective-permute-done((bf16[4,64,192]{2,1,0:T(8,128)(2,1)S(1)}, bf16[4,64,192]{2,1,0:T(8,128)(2,1)S(1)}, u32[]{:S(2)}, u32[]{:S(2)}) %collective-permute-start.2) | collective-permute-done | bytes 98336 | tf_op jit(solution)/shard_map/ppermute | solution.py:341
  43.2 3.3 %collective-permute-done.7.c3 = bf16[4,64,192]{2,1,0:T(8,128)(2,1)S(1)} collective-permute-done((bf16[4,64,192]{2,1,0:T(8,128)(2,1)S(1)}, bf16[4,64,192]{2,1,0:T(8,128)(2,1)S(1)}, u32[]{:S(2)}, u32[]{:S(2)}) %collective-permute-start.7) | collective-permute-done | bytes 98336 | tf_op jit(solution)/shard_map/ppermute | solution.py:342
  46.6 0.0 copy-done.3
  46.6 0.0 copy-done.6
  46.6 0.0 copy-done.1
  46.6 0.0 copy-done.7
  46.6 0.0 copy-done.2
  46.6 0.0 copy-start.8
  46.6 0.6 copy-done.8
  47.3 18.9 %spectra.1 = f32[64,192]{1,0:T(8,128)} custom-call(s32[2]{0:T(128)} %pad_add_fusion.place_ref, f32[1024,512]{1,0:T(8,128)} %cos_ref.1, bf16[1,64,192]{2,1,0:T(8,128)(2,1)} %bitcast.9, bf16[1,64,192]{2,1,0:T(8,128)(2,1)} %copy-done.3, bf16[2,64,192]{2,1,0:T(8,128)(2,1)} %copy-done.1, bf16[4,64,192]{2,1,0:T(8,128)(2,1)} %copy-done.2, ...), custom_call_target="tpu_custom_call" | custom-call | flops 8999999488 | bytes 4000000 | tf_op jit(solution)/shard_map/spectra/pallas_call | solution.py:297
  66.2 0.0 collective-permute-start.8
  66.2 1.5 %collective-permute-done.8 = f32[64,192]{1,0:T(8,128)S(1)} collective-permute-done((f32[64,192]{1,0:T(8,128)}, f32[64,192]{1,0:T(8,128)S(1)}, u32[]{:S(2)}, u32[]{:S(2)}) %collective-permute-start.8) | collective-permute-done | bytes 49184 | tf_op jit(solution)/shard_map/ppermute | solution.py:326
  67.6 0.9 add.29
  68.5 0.1 collective-permute-start.9
  68.6 4.3 %collective-permute-done.9 = f32[64,192]{1,0:T(8,128)S(1)} collective-permute-done((f32[64,192]{1,0:T(8,128)S(1)}, f32[64,192]{1,0:T(8,128)S(1)}, u32[]{:S(2)}, u32[]{:S(2)}) %collective-permute-start.9) | collective-permute-done | bytes 49184 | tf_op jit(solution)/shard_map/ppermute | solution.py:328
  72.9 0.1 collective-permute-start.10
  72.9 5.5 %collective-permute-done.10 = f32[64,192]{1,0:T(8,128)S(1)} collective-permute-done((f32[64,192]{1,0:T(8,128)S(1)}, f32[64,192]{1,0:T(8,128)S(1)}, u32[]{:S(2)}, u32[]{:S(2)}) %collective-permute-start.10) | collective-permute-done | bytes 49184 | tf_op jit(solution)/shard_map/ppermute | solution.py:329
  78.4 0.1 collective-permute-start.11
  78.5 1.0 pad_maximum_fusion
  79.5 1.6 %collective-permute-start.3 = (bf16[8,64,192]{2,1,0:T(8,128)(2,1)S(1)}, bf16[8,64,192]{2,1,0:T(8,128)(2,1)S(1)}, u32[]{:S(2)}, u32[]{:S(2)}) collective-permute-start(bf16[8,64,192]{2,1,0:T(8,128)(2,1)S(1)} %pad_maximum_fusion), channel_id=1, source_target_pairs={{1,0},{2,3},{4,5},{6,7},{8,9},{10,11},{12,13},{14,15},{0,1},{3,2},... | collective-permute-start | bytes 589832 | tf_op jit(solution)/shard_map/ppermute | solution.py:343
  81.0 1.7 %collective-permute-done.11 = f32[64,192]{1,0:T(8,128)S(1)} collective-permute-done((f32[64,192]{1,0:T(8,128)S(1)}, f32[64,192]{1,0:T(8,128)S(1)}, u32[]{:S(2)}, u32[]{:S(2)}) %collective-permute-start.11) | collective-permute-done | bytes 49184 | tf_op jit(solution)/shard_map/ppermute | solution.py:328
  82.8 0.2 collective-permute-start.12
  83.0 5.4 %collective-permute-done.12 = f32[64,192]{1,0:T(8,128)S(1)} collective-permute-done((f32[64,192]{1,0:T(8,128)S(1)}, f32[64,192]{1,0:T(8,128)S(1)}, u32[]{:S(2)}, u32[]{:S(2)}) %collective-permute-start.12) | collective-permute-done | bytes 49184 | tf_op jit(solution)/shard_map/ppermute | solution.py:329
  88.4 1.6 %collective-permute-start.13 = (f32[64,192]{1,0:T(8,128)S(1)}, f32[64,192]{1,0:T(8,128)S(1)}, u32[]{:S(2)}, u32[]{:S(2)}) collective-permute-start(f32[64,192]{1,0:T(8,128)S(1)} %add.33), channel_id=1, source_target_pairs={{0,1},{1,0},{2,3},{3,2},{4,5},{5,4},{6,7},{7,6},{8,9},{9,8},{10,11... | collective-permute-start | bytes 147464 | tf_op jit(solution)/shard_map/ppermute | solution.py:328
  89.9 2.8 %collective-permute-done.13 = f32[64,192]{1,0:T(8,128)S(1)} collective-permute-done((f32[64,192]{1,0:T(8,128)S(1)}, f32[64,192]{1,0:T(8,128)S(1)}, u32[]{:S(2)}, u32[]{:S(2)}) %collective-permute-start.13) | collective-permute-done | bytes 49184 | tf_op jit(solution)/shard_map/ppermute | solution.py:328
  92.7 0.1 collective-permute-start.14
  92.8 0.0 collective-permute-done.3.other_ref
  92.8 0.7 copy-done.4
  93.5 2.1 %assemble.1 = bf16[192,1024]{1,0:T(8,128)(2,1)} custom-call(s32[2]{0:T(128)} %pad_add_fusion.place_ref, bf16[1,64,192]{2,1,0:T(8,128)(2,1)} %bitcast.11, bf16[1,64,192]{2,1,0:T(8,128)(2,1)} %copy-done.3, bf16[2,64,192]{2,1,0:T(8,128)(2,1)} %copy-done.1, bf16[4,64,192]{2,1,0:T(8,128)(2,1)} %copy-done.2, bf16[8,64,192]{2,1,0:T(8,128)(2,1)} %copy-done.4), custom_call_target="tpu_custom_call" | custom-call | tf_op jit(solution)/shard_map/assemble/pallas_call | solution.py:315
  95.6 2.7 %collective-permute-done.14 = f32[64,192]{1,0:T(8,128)S(1)} collective-permute-done((f32[64,192]{1,0:T(8,128)S(1)}, f32[64,192]{1,0:T(8,128)S(1)}, u32[]{:S(2)}, u32[]{:S(2)}) %collective-permute-start.14) | collective-permute-done | bytes 49184 | tf_op jit(solution)/shard_map/ppermute | solution.py:329
  98.3 0.6 add.35
  (19 shorter events, 0.1 us)
Async XLA Ops:
  24.6 22.0 %copy-start = (bf16[64,192]{1,0:T(8,128)(2,1)}, bf16[64,192]{1,0:T(8,128)(2,1)S(1)}, u32[]{:S(2)}) copy-start(bf16[64,192]{1,0:T(8,128)(2,1)S(1)} %convert_reduce_fusion) | copy-start | bytes 73732
  24.6 4.0 %collective-permute-start.4 = (bf16[64,192]{1,0:T(8,128)(2,1)S(1)}, bf16[64,192]{1,0:T(8,128)(2,1)S(1)}, u32[]{:S(2)}, u32[]{:S(2)}) collective-permute-start(bf16[64,192]{1,0:T(8,128)(2,1)S(1)} %convert_reduce_fusion), channel_id=1, source_target_pairs={{1,0},{2,16},{4,32},{6,48},{8,64},{10,80},{12,96},{14,112},{0,1},{... | collective-permute-start | bytes 73736 | tf_op jit(solution)/shard_map/ppermute | solution.py:339
  25.3 5.1 %collective-permute-start = (bf16[1,64,192]{2,1,0:T(8,128)(2,1)S(1)}, bf16[1,64,192]{2,1,0:T(8,128)(2,1)S(1)}, u32[]{:S(2)}, u32[]{:S(2)}) collective-permute-start(bf16[1,64,192]{2,1,0:T(8,128)(2,1)S(1)} %bitcast.6), channel_id=1, source_target_pairs={{1,2},{2,1},{4,6},{6,4},{8,10},{10,8},{12,14},{14,12},{0,3},{3,0},... | collective-permute-start | bytes 73736 | tf_op jit(solution)/shard_map/ppermute | solution.py:341
  28.6 18.0 %copy-start.5 = (bf16[64,192]{1,0:T(8,128)(2,1)}, bf16[64,192]{1,0:T(8,128)(2,1)S(1)}, u32[]{:S(2)}) copy-start(bf16[64,192]{1,0:T(8,128)(2,1)S(1)} %collective-permute-done.4) | copy-start | bytes 73732
  28.6 4.6 %collective-permute-start.5 = (bf16[1,64,192]{2,1,0:T(8,128)(2,1)S(1)}, bf16[1,64,192]{2,1,0:T(8,128)(2,1)S(1)}, u32[]{:S(2)}, u32[]{:S(2)}) collective-permute-start(bf16[1,64,192]{2,1,0:T(8,128)(2,1)S(1)} %bitcast.14), channel_id=1, source_target_pairs={{0,16},{1,17},{2,18},{3,19},{4,20},{5,21},{6,22},{7,23},{8,24},{9,... | collective-permute-start | bytes 73736 | tf_op jit(solution)/shard_map/ppermute | solution.py:342
  30.4 16.2 %copy-start.3 = (bf16[1,64,192]{2,1,0:T(8,128)(2,1)}, bf16[1,64,192]{2,1,0:T(8,128)(2,1)S(1)}, u32[]{:S(2)}) copy-start(bf16[1,64,192]{2,1,0:T(8,128)(2,1)S(1)} %collective-permute-done.r1) | copy-start | bytes 73732
  30.4 5.2 %collective-permute-start.1 = (bf16[2,64,192]{2,1,0:T(8,128)(2,1)S(1)}, bf16[2,64,192]{2,1,0:T(8,128)(2,1)S(1)}, u32[]{:S(2)}, u32[]{:S(2)}) collective-permute-start(bf16[2,64,192]{2,1,0:T(8,128)(2,1)S(1)} %pad_maximum_fusion.3), channel_id=1, source_target_pairs={{1,4},{2,6},{4,1},{6,2},{8,12},{10,14},{12,8},{14,10},{0,5},{3,7},... | collective-permute-start | bytes 147464 | tf_op jit(solution)/shard_map/ppermute | solution.py:341
  33.3 13.3 %copy-start.6 = (bf16[1,64,192]{2,1,0:T(8,128)(2,1)}, bf16[1,64,192]{2,1,0:T(8,128)(2,1)S(1)}, u32[]{:S(2)}) copy-start(bf16[1,64,192]{2,1,0:T(8,128)(2,1)S(1)} %collective-permute-done.5.c1) | copy-start | bytes 73732
  33.3 7.0 %collective-permute-start.6 = (bf16[2,64,192]{2,1,0:T(8,128)(2,1)S(1)}, bf16[2,64,192]{2,1,0:T(8,128)(2,1)S(1)}, u32[]{:S(2)}, u32[]{:S(2)}) collective-permute-start(bf16[2,64,192]{2,1,0:T(8,128)(2,1)S(1)} %pad_maximum_fusion.4), channel_id=1, source_target_pairs={{0,32},{1,33},{2,34},{3,35},{4,36},{5,37},{6,38},{7,39},{8,40},{9,... | collective-permute-start | bytes 147464 | tf_op jit(solution)/shard_map/ppermute | solution.py:342
  35.7 10.9 %copy-start.1 = (bf16[2,64,192]{2,1,0:T(8,128)(2,1)}, bf16[2,64,192]{2,1,0:T(8,128)(2,1)S(1)}, u32[]{:S(2)}) copy-start(bf16[2,64,192]{2,1,0:T(8,128)(2,1)S(1)} %collective-permute-done.1.r2) | copy-start | bytes 147460
  35.7 7.5 %collective-permute-start.2 = (bf16[4,64,192]{2,1,0:T(8,128)(2,1)S(1)}, bf16[4,64,192]{2,1,0:T(8,128)(2,1)S(1)}, u32[]{:S(2)}, u32[]{:S(2)}) collective-permute-start(bf16[4,64,192]{2,1,0:T(8,128)(2,1)S(1)} %pad_maximum_fusion.1), channel_id=1, source_target_pairs={{1,12},{2,14},{4,8},{6,10},{8,4},{10,6},{12,1},{14,2},{0,13},{3,15... | collective-permute-start | bytes 294920 | tf_op jit(solution)/shard_map/ppermute | solution.py:341
  40.3 6.3 %copy-start.7 = (bf16[2,64,192]{2,1,0:T(8,128)(2,1)}, bf16[2,64,192]{2,1,0:T(8,128)(2,1)S(1)}, u32[]{:S(2)}) copy-start(bf16[2,64,192]{2,1,0:T(8,128)(2,1)S(1)} %collective-permute-done.6.c2) | copy-start | bytes 147460
  40.3 6.3 %collective-permute-start.7 = (bf16[4,64,192]{2,1,0:T(8,128)(2,1)S(1)}, bf16[4,64,192]{2,1,0:T(8,128)(2,1)S(1)}, u32[]{:S(2)}, u32[]{:S(2)}) collective-permute-start(bf16[4,64,192]{2,1,0:T(8,128)(2,1)S(1)} %pad_maximum_fusion.2), channel_id=1, source_target_pairs={{0,96},{1,97},{2,98},{3,99},{4,100},{5,101},{6,102},{7,103},{8,104... | collective-permute-start | bytes 294920 | tf_op jit(solution)/shard_map/ppermute | solution.py:342
  43.2 3.4 %copy-start.2 = (bf16[4,64,192]{2,1,0:T(8,128)(2,1)}, bf16[4,64,192]{2,1,0:T(8,128)(2,1)S(1)}, u32[]{:S(2)}) copy-start(bf16[4,64,192]{2,1,0:T(8,128)(2,1)S(1)} %collective-permute-done.2.r3) | copy-start | bytes 294916
  46.6 0.7 copy-start.8
  66.2 1.5 %collective-permute-start.8 = (f32[64,192]{1,0:T(8,128)}, f32[64,192]{1,0:T(8,128)S(1)}, u32[]{:S(2)}, u32[]{:S(2)}) collective-permute-start(f32[64,192]{1,0:T(8,128)} %spectra.1), channel_id=1, source_target_pairs={{0,16},{16,0},{1,17},{17,1},{2,18},{18,2},{3,19},{19,3},{4,20},{20... | collective-permute-start | bytes 147464 | tf_op jit(solution)/shard_map/ppermute | solution.py:326
  68.5 4.3 %collective-permute-start.9 = (f32[64,192]{1,0:T(8,128)S(1)}, f32[64,192]{1,0:T(8,128)S(1)}, u32[]{:S(2)}, u32[]{:S(2)}) collective-permute-start(f32[64,192]{1,0:T(8,128)S(1)} %add.29), channel_id=1, source_target_pairs={{0,32},{32,0},{64,96},{96,64},{1,33},{33,1},{65,97},{97,65},{2,34}... | collective-permute-start | bytes 147464 | tf_op jit(solution)/shard_map/ppermute | solution.py:328
  72.9 5.6 %collective-permute-start.10 = (f32[64,192]{1,0:T(8,128)S(1)}, f32[64,192]{1,0:T(8,128)S(1)}, u32[]{:S(2)}, u32[]{:S(2)}) collective-permute-start(f32[64,192]{1,0:T(8,128)S(1)} %add.30), channel_id=1, source_target_pairs={{0,96},{96,0},{64,32},{32,64},{1,97},{97,1},{65,33},{33,65},{2,98}... | collective-permute-start | bytes 147464 | tf_op jit(solution)/shard_map/ppermute | solution.py:329
  78.4 4.3 %collective-permute-start.11 = (f32[64,192]{1,0:T(8,128)S(1)}, f32[64,192]{1,0:T(8,128)S(1)}, u32[]{:S(2)}, u32[]{:S(2)}) collective-permute-start(f32[64,192]{1,0:T(8,128)S(1)} %add.31), channel_id=1, source_target_pairs={{0,4},{4,0},{8,12},{12,8},{1,5},{5,1},{9,13},{13,9},{2,6},{6,2},{1... | collective-permute-start | bytes 147464 | tf_op jit(solution)/shard_map/ppermute | solution.py:328
  79.5 13.3 %collective-permute-start.3 = (bf16[8,64,192]{2,1,0:T(8,128)(2,1)S(1)}, bf16[8,64,192]{2,1,0:T(8,128)(2,1)S(1)}, u32[]{:S(2)}, u32[]{:S(2)}) collective-permute-start(bf16[8,64,192]{2,1,0:T(8,128)(2,1)S(1)} %pad_maximum_fusion), channel_id=1, source_target_pairs={{1,0},{2,3},{4,5},{6,7},{8,9},{10,11},{12,13},{14,15},{0,1},{3,2},... | collective-permute-start | bytes 589832 | tf_op jit(solution)/shard_map/ppermute | solution.py:343
  82.8 5.6 %collective-permute-start.12 = (f32[64,192]{1,0:T(8,128)S(1)}, f32[64,192]{1,0:T(8,128)S(1)}, u32[]{:S(2)}, u32[]{:S(2)}) collective-permute-start(f32[64,192]{1,0:T(8,128)S(1)} %add.32), channel_id=1, source_target_pairs={{0,12},{12,0},{8,4},{4,8},{1,13},{13,1},{9,5},{5,9},{2,14},{14,2},... | collective-permute-start | bytes 147464 | tf_op jit(solution)/shard_map/ppermute | solution.py:329
  88.4 4.3 %collective-permute-start.13 = (f32[64,192]{1,0:T(8,128)S(1)}, f32[64,192]{1,0:T(8,128)S(1)}, u32[]{:S(2)}, u32[]{:S(2)}) collective-permute-start(f32[64,192]{1,0:T(8,128)S(1)} %add.33), channel_id=1, source_target_pairs={{0,1},{1,0},{2,3},{3,2},{4,5},{5,4},{6,7},{7,6},{8,9},{9,8},{10,11... | collective-permute-start | bytes 147464 | tf_op jit(solution)/shard_map/ppermute | solution.py:328
  92.7 5.6 %collective-permute-start.14 = (f32[64,192]{1,0:T(8,128)S(1)}, f32[64,192]{1,0:T(8,128)S(1)}, u32[]{:S(2)}, u32[]{:S(2)}) collective-permute-start(f32[64,192]{1,0:T(8,128)S(1)} %add.34), channel_id=1, source_target_pairs={{0,3},{3,0},{2,1},{1,2},{4,7},{7,4},{6,5},{5,6},{8,11},{11,8},{10,... | collective-permute-start | bytes 147464 | tf_op jit(solution)/shard_map/ppermute | solution.py:329
  92.8 0.7 copy-start.4
